TPU v7x, 128 devices: a whole 4x4x4 slice. The times are simulated.
128 devices in a mesh: dom: 128 (over y, z, x, core).
Axes of the slice: x: 4, y: 4, z: 4, core: 2. Of those that a mesh axis runs over, the one named last changes fastest.
Arguments:
- concentration: float32 [4096, 128], P('dom'), may hold values from 0 to 1
- reaction_rate: float32 [4096, 128], P('dom'), may hold values from 0.5 to 4
- step_size: float32 [1], replicated, may hold values from 1 to 2
- block_values: float32 [4096, 5, 128, 128], P('dom'), may hold values from -40 to 48, as said below
- block_columns: int32 [4096, 5], P('dom'), may hold values from 0 to 95, as said below
- row_lengths: int32 [4096], P('dom'), may hold values from 2 to 5, as said below
- send_lists: int32 [128, 4, 16], P('dom'), may hold values from 0 to 31, as said below
Outputs:
- next_concentration: float32 [4096, 128], P('dom')
Inputs may be any that keep to these rules, and one draw needn't show every extreme that they name: `send_lists`: for every partition and offset index q (offsets -2, -1, +1, +2), 16 distinct local block indices. `block_columns`: slot 0 of a block row is the row's own local block; live slots name a local block (below 32) or a ghost slot 32 + q * 16 + g of a block that the partition at offset index q sends; slot 1 of local block row q, for q = 0..3, is a ghost slot of offset index q; slots at or past the row's length repeat the row's own local block. `row_lengths`: some block row has all 5 slots live. `block_values`: slot 0 of every block row holds 8 times the identity plus a full random block; the other slots hold full random blocks.
All inputs are finite; a program needn't handle non-finite values.
Results may differ from a plain program's by a relative error of at most 0.00016.
Values sent between devices are 32-bit elements; how exact they have to be, the bound alone decides.
A program may use at most 64 MiB of HBM per device.

v0:
```python
import jax
import jax.numpy as jnp
from jax import lax
from jax.sharding import Mesh
from jax.sharding import PartitionSpec as P

KRYLOV = 3
RESTARTS = 2
DOM = ("dom_0", "dom_1", "dom_2", "dom_3")


epsilon = 1e-06


def passed_along(value, axis, by):
    length = lax.axis_size(axis)
    return lax.ppermute(value, axis, [(i, (i + by) % length) for i in range(length)])


def from_everyone(value, axis):
    copies = jnp.broadcast_to(value, (lax.axis_size(axis), *value.shape))
    return lax.all_to_all(copies, axis, split_axis=0, concat_axis=0, tiled=True)


def over_copies(value, axis):
    everything = from_everyone(value, axis)
    return jnp.sum(everything, axis=0)


def one_axis_at_a_time(value, axes):
    far, near = axes
    nearer = over_copies(value, near)
    return over_copies(nearer, far)


def in_one(arrays, axis):
    line, at, done = (jnp.concatenate([a.reshape(-1) for a in arrays]), 0, [])
    total = one_axis_at_a_time(line, axis)
    for a in arrays:
        done.append(total[at : at + a.size].reshape(a.shape))
        at += a.size
    return tuple(done)


def extend_field(field, send_lists):
    packets = field[send_lists[0]]
    from_minus_two = passed_along(packets[0], DOM, -2)
    from_minus_one = passed_along(packets[1], DOM, -1)
    from_plus_one = passed_along(packets[2], DOM, 1)
    from_plus_two = passed_along(packets[3], DOM, 2)
    ghosts = [from_minus_two, from_minus_one, from_plus_one, from_plus_two]
    return jnp.concatenate([field] + ghosts, axis=0)


def product(block_values, block_columns, active, send_lists, field):
    extended = extend_field(field, send_lists)
    gathered = extended[block_columns] * active[:, :, None]
    return jnp.einsum("bsij,bsj->bi", block_values, gathered, precision=lax.Precision.HIGHEST)


def phi_column(hessenberg, substep):
    order = hessenberg.shape[0]
    augmented = jnp.zeros((order + 1, order + 1), jnp.float32)
    augmented = augmented.at[:order, :order].set(substep * hessenberg).at[0, order].set(1.0)
    reduced = augmented / 64.0
    identity = jnp.eye(order + 1, dtype=jnp.float32)
    series = identity
    for degree in range(12, 0, -1):
        series = identity + jnp.dot(reduced, series, precision=lax.Precision.HIGHEST) / degree
    for square_turn in range(6):
        series = jnp.dot(series, series, precision=lax.Precision.HIGHEST)
    return series[:order, order]


def local_dots(vectors, mapped):
    return jnp.einsum("kbi,bi->k", vectors, mapped, precision=lax.Precision.HIGHEST)


def combine(weights, vectors):
    return jnp.einsum("k,kbi->bi", weights, vectors, precision=lax.Precision.HIGHEST)


def krylov(start, apply):
    squared = one_axis_at_a_time(jnp.sum(start * start), (("dom_0", "dom_1", "dom_2"), "dom_3"))
    magnitude = jnp.sqrt(squared + epsilon)
    vectors = jnp.zeros((KRYLOV,) + start.shape, jnp.float32).at[0].set(start / magnitude)
    hessenberg = jnp.zeros((KRYLOV, KRYLOV), jnp.float32)
    mapped = apply(vectors[0])
    projection = one_axis_at_a_time(
        local_dots(vectors, mapped), (("dom_0", "dom_1", "dom_2"), "dom_3")
    )
    residue = mapped - combine(projection, vectors)
    hessenberg = hessenberg.at[:, 0].set(projection)
    for column in range(1, KRYLOV):
        mapped = apply(residue)
        inner, self_term, residue_square = in_one(
            (local_dots(vectors, mapped), jnp.sum(residue * mapped), jnp.sum(residue * residue)),
            (("dom_0", "dom_1", "dom_2"), "dom_3"),
        )
        length = jnp.sqrt(residue_square + epsilon)
        vectors = vectors.at[column].set(residue / length)
        projection = (inner / length).at[column].set(self_term / (length * length))
        hessenberg = hessenberg.at[column, column - 1].set(length).at[:, column].set(projection)
        residue = mapped / length - combine(projection, vectors)
    return (magnitude, vectors, hessenberg)


def shards(
    concentration, reaction_rate, step_size, block_values, block_columns, row_lengths, send_lists
):
    slot_count = block_columns.shape[1]
    active = (jnp.arange(slot_count, dtype=jnp.int32)[None, :] < row_lengths[:, None]).astype(
        jnp.float32
    )
    slope = reaction_rate * (1.0 - 2.0 * concentration)

    def operator(field):
        return product(block_values, block_columns, active, send_lists, field)

    def apply(field):
        return slope * field - operator(field)

    forcing = reaction_rate * concentration * (1.0 - concentration) - operator(concentration)
    substep = step_size[0] / RESTARTS
    increment = jnp.zeros_like(concentration)
    for restart in range(RESTARTS):
        start = forcing if restart == 0 else apply(increment) + forcing
        magnitude, vectors, hessenberg = krylov(start, apply)
        weights = phi_column(hessenberg, substep)
        increment = increment + substep * magnitude * combine(weights, vectors)
    return concentration + increment


def solution(mesh):
    torus = Mesh(mesh.devices.reshape(4, 4, 4, 2), ("dom_0", "dom_1", "dom_2", "dom_3"))
    placed = (
        P(DOM, None),
        P(DOM, None),
        P(),
        P(DOM, None, None, None),
        P(DOM, None),
        P(DOM),
        P(DOM, None, None),
    )
    return jax.shard_map(
        shards, mesh=torus, in_specs=placed, out_specs=P(DOM, None), check_vma=False
    )
```

profile of v0, /device:TPU:1, one launch (start us, length us, event | category | flops | bytes accessed | tf_op | source)
XLA Modules:
  0.0 407.9 jit_solution(3137005875486056520)
XLA Ops:
  2.1 9.3 %collective-permute-start = (f32[16,128]{1,0:T(8,128)S(1)}, f32[16,128]{1,0:T(8,128)S(1)}, u32[]{:S(2)}, u32[]{:S(2)}) collective-permute-start(f32[16,128]{1,0:T(8,128)S(1)} %get-tuple-element.356), channel_id=1, source_target_pairs={{0,126},{1,127},{2,0},{3,1},{4,2},{5,3},{6,4},{7,5},{8,6},{9,7},{1... | collective-permute-start | bytes 24584 | tf_op jit(solution)/shard_map/ppermute | solution.py:17
  15.6 5.5 %collective-permute-done.3 = f32[16,128]{1,0:T(8,128)S(1)} collective-permute-done((f32[16,128]{1,0:T(8,128)S(1)}, f32[16,128]{1,0:T(8,128)S(1)}, u32[]{:S(2)}, u32[]{:S(2)}) %collective-permute-start.3) | collective-permute-done | bytes 8224 | tf_op jit(solution)/shard_map/ppermute | solution.py:17
  21.9 12.6 %fusion.36 = f32[32,1,128,1]{2,1,3,0:T(1,128)S(1)} fusion(f32[32,5,128,128]{3,2,1,0:T(8,128)} %param.58, f32[32,5,128,1]{2,1,0,3:T(8,128)S(1)} %multiply_bitcast_fusion.7), kind=kOutput, calls=%fused_computation.132 | convolution fusion | flops 31457280 | bytes 10584064 | tf_op jit(solution)/shard_map/bsij,bsj->bi/dot_general | solution.py:58
  35.8 4.2 %all_to_all.96 = f32[2,1,1]{2,1,0:T(1,128)S(1)} all-to-all(f32[2,1,1]{2,1,0:T(1,128)S(1)} %broadcast_in_dim.35), channel_id=1, replica_groups=mesh['dom_0'=4,'dom_1'=4,'dom_2'=4,'dom_3'=2] {'dom_3'}, dimensions={0} | all-to-all | bytes 16 | tf_op jit(solution)/shard_map/all_to_all | solution.py:22
  41.3 12.2 %all_to_all.97 = f32[64,1,1]{2,1,0:T(1,128)S(1)} all-to-all(f32[64,1,1]{2,1,0:T(1,128)S(1)} %broadcast_in_dim.36), channel_id=1, replica_groups=mesh['dom_0'=4,'dom_1'=4,'dom_2'=4,'dom_3'=2] {'dom_0','dom_1','dom_2'}, dimensions={0} | all-to-all | bytes 512 | tf_op jit(solution)/shard_map/all_to_all | solution.py:22
  55.5 2.1 collective-permute-start.4
  60.8 6.8 %collective-permute-done.7 = f32[16,128]{1,0:T(8,128)S(1)} collective-permute-done((f32[16,128]{1,0:T(8,128)S(1)}, f32[16,128]{1,0:T(8,128)S(1)}, u32[]{:S(2)}, u32[]{:S(2)}) %collective-permute-start.7) | collective-permute-done | bytes 8224 | tf_op jit(solution)/shard_map/ppermute | solution.py:17
  68.4 12.6 %fusion.34 = f32[32,1,128,1]{2,1,3,0:T(1,128)S(1)} fusion(f32[32,5,128,128]{3,2,1,0:T(8,128)} %param.58, f32[32,5,128,1]{2,1,0,3:T(8,128)S(1)} %multiply_bitcast_fusion.6), kind=kOutput, calls=%fused_computation.130 | convolution fusion | flops 31457280 | bytes 10584064 | tf_op jit(solution)/shard_map/bsij,bsj->bi/dot_general | solution.py:58
  81.4 5.0 %all_to_all.98 = f32[2,1,3]{2,1,0:T(1,128)S(1)} all-to-all(f32[2,1,3]{2,1,0:T(1,128)S(1)} %broadcast_in_dim.37), channel_id=1, replica_groups=mesh['dom_0'=4,'dom_1'=4,'dom_2'=4,'dom_3'=2] {'dom_3'}, dimensions={0} | all-to-all | bytes 48 | tf_op jit(solution)/shard_map/all_to_all | solution.py:22
  86.5 12.2 %all_to_all.99 = f32[64,1,3]{2,1,0:T(1,128)S(1)} all-to-all(f32[64,1,3]{2,1,0:T(1,128)S(1)} %broadcast_in_dim.38), channel_id=1, replica_groups=mesh['dom_0'=4,'dom_1'=4,'dom_2'=4,'dom_3'=2] {'dom_0','dom_1','dom_2'}, dimensions={0} | all-to-all | bytes 1536 | tf_op jit(solution)/shard_map/all_to_all | solution.py:22
  99.7 2.1 collective-permute-start.8
  104.9 6.8 %collective-permute-done.11 = f32[16,128]{1,0:T(8,128)S(1)} collective-permute-done((f32[16,128]{1,0:T(8,128)S(1)}, f32[16,128]{1,0:T(8,128)S(1)}, u32[]{:S(2)}, u32[]{:S(2)}) %collective-permute-start.11) | collective-permute-done | bytes 8224 | tf_op jit(solution)/shard_map/ppermute | solution.py:17
  112.5 12.6 %fusion.32 = f32[32,1,128,1]{2,1,3,0:T(1,128)S(1)} fusion(f32[32,5,128,128]{3,2,1,0:T(8,128)} %param.58, f32[32,5,128,1]{2,1,0,3:T(8,128)S(1)} %multiply_bitcast_fusion.5), kind=kOutput, calls=%fused_computation.128 | convolution fusion | flops 31457280 | bytes 10584064 | tf_op jit(solution)/shard_map/bsij,bsj->bi/dot_general | solution.py:58
  127.7 5.2 %all_to_all.100 = f32[2,1,5]{2,1,0:T(1,128)S(1)} all-to-all(f32[2,1,5]{2,1,0:T(1,128)S(1)} %broadcast_in_dim.39), channel_id=1, replica_groups=mesh['dom_0'=4,'dom_1'=4,'dom_2'=4,'dom_3'=2] {'dom_3'}, dimensions={0} | all-to-all | bytes 80 | tf_op jit(solution)/shard_map/all_to_all | solution.py:22
  133.5 4.6 %all-to-all-start.5 = ((f32[64,1,5]{2,1,0:T(1,128)}), f32[64,1,5]{2,1,0:T(1,128)S(1)}, u32[]{:S(2)}, u32[]{:S(2)}) async-start(f32[64,1,5]{2,1,0:T(1,128)} %broadcast_in_dim.40), calls=%async_computation.5 | async-start | bytes 65536 | tf_op jit(solution)/shard_map/all_to_all | solution.py:22
  141.4 5.2 %all-to-all-done.5 = f32[64,1,5]{2,1,0:T(1,128)S(1)} async-done(((f32[64,1,5]{2,1,0:T(1,128)}), f32[64,1,5]{2,1,0:T(1,128)S(1)}, u32[]{:S(2)}, u32[]{:S(2)}) %all-to-all-start.5) | async-done | bytes 1312 | tf_op jit(solution)/shard_map/all_to_all | solution.py:22
  149.6 2.1 collective-permute-start.12
  155.5 6.9 %collective-permute-done.15 = f32[16,128]{1,0:T(8,128)S(1)} collective-permute-done((f32[16,128]{1,0:T(8,128)S(1)}, f32[16,128]{1,0:T(8,128)S(1)}, u32[]{:S(2)}, u32[]{:S(2)}) %collective-permute-start.15) | collective-permute-done | bytes 8224 | tf_op jit(solution)/shard_map/ppermute | solution.py:17
  163.2 12.6 %fusion.30 = f32[32,1,128,1]{2,1,3,0:T(1,128)S(1)} fusion(f32[32,5,128,128]{3,2,1,0:T(8,128)} %param.58, f32[32,5,128,1]{2,1,0,3:T(8,128)S(1)} %multiply_bitcast_fusion.4), kind=kOutput, calls=%fused_computation.126 | convolution fusion | flops 31457280 | bytes 10584064 | tf_op jit(solution)/shard_map/bsij,bsj->bi/dot_general | solution.py:58
  178.3 4.7 %all_to_all.101 = f32[2,1,5]{2,1,0:T(1,128)S(1)} all-to-all(f32[2,1,5]{2,1,0:T(1,128)S(1)} %broadcast_in_dim.41), channel_id=1, replica_groups=mesh['dom_0'=4,'dom_1'=4,'dom_2'=4,'dom_3'=2] {'dom_3'}, dimensions={0} | all-to-all | bytes 80 | tf_op jit(solution)/shard_map/all_to_all | solution.py:22
  183.7 4.6 %all-to-all-start.7 = ((f32[64,1,5]{2,1,0:T(1,128)}), f32[64,1,5]{2,1,0:T(1,128)S(1)}, u32[]{:S(2)}, u32[]{:S(2)}) async-start(f32[64,1,5]{2,1,0:T(1,128)} %broadcast_in_dim.84), calls=%async_computation.7 | async-start | bytes 65536 | tf_op jit(solution)/shard_map/all_to_all | solution.py:22
  188.9 7.8 %all-to-all-done.7 = f32[64,1,5]{2,1,0:T(1,128)S(1)} async-done(((f32[64,1,5]{2,1,0:T(1,128)}), f32[64,1,5]{2,1,0:T(1,128)S(1)}, u32[]{:S(2)}, u32[]{:S(2)}) %all-to-all-start.7) | async-done | bytes 1312 | tf_op jit(solution)/shard_map/all_to_all | solution.py:22
  199.1 2.6 fusion.80
  201.6 2.0 scatter.96
  207.9 2.1 collective-permute-start.16
  213.2 6.8 %collective-permute-done.19 = f32[16,128]{1,0:T(8,128)S(1)} collective-permute-done((f32[16,128]{1,0:T(8,128)S(1)}, f32[16,128]{1,0:T(8,128)S(1)}, u32[]{:S(2)}, u32[]{:S(2)}) %collective-permute-start.19) | collective-permute-done | bytes 8224 | tf_op jit(solution)/shard_map/ppermute | solution.py:17
  220.7 12.6 %fusion.28 = f32[32,1,128,1]{2,1,3,0:T(1,128)S(1)} fusion(f32[32,5,128,128]{3,2,1,0:T(8,128)} %param.58, f32[32,5,128,1]{2,1,0,3:T(8,128)S(1)} %multiply_bitcast_fusion.3), kind=kOutput, calls=%fused_computation.124 | convolution fusion | flops 31457280 | bytes 10584064 | tf_op jit(solution)/shard_map/bsij,bsj->bi/dot_general | solution.py:58
  234.8 5.0 %all_to_all.102 = f32[2,1,1]{2,1,0:T(1,128)S(1)} all-to-all(f32[2,1,1]{2,1,0:T(1,128)S(1)} %broadcast_in_dim.85), channel_id=1, replica_groups=mesh['dom_0'=4,'dom_1'=4,'dom_2'=4,'dom_3'=2] {'dom_3'}, dimensions={0} | all-to-all | bytes 16 | tf_op jit(solution)/shard_map/all_to_all | solution.py:22
  241.2 12.2 %all_to_all.103 = f32[64,1,1]{2,1,0:T(1,128)S(1)} all-to-all(f32[64,1,1]{2,1,0:T(1,128)S(1)} %broadcast_in_dim.86), channel_id=1, replica_groups=mesh['dom_0'=4,'dom_1'=4,'dom_2'=4,'dom_3'=2] {'dom_0','dom_1','dom_2'}, dimensions={0} | all-to-all | bytes 512 | tf_op jit(solution)/shard_map/all_to_all | solution.py:22
  255.5 2.1 collective-permute-start.20
  260.7 6.8 %collective-permute-done.23 = f32[16,128]{1,0:T(8,128)S(1)} collective-permute-done((f32[16,128]{1,0:T(8,128)S(1)}, f32[16,128]{1,0:T(8,128)S(1)}, u32[]{:S(2)}, u32[]{:S(2)}) %collective-permute-start.23) | collective-permute-done | bytes 8224 | tf_op jit(solution)/shard_map/ppermute | solution.py:17
  268.3 12.6 %fusion.26 = f32[32,1,128,1]{2,1,3,0:T(1,128)S(1)} fusion(f32[32,5,128,128]{3,2,1,0:T(8,128)} %param.58, f32[32,5,128,1]{2,1,0,3:T(8,128)S(1)} %multiply_bitcast_fusion.2), kind=kOutput, calls=%fused_computation.122 | convolution fusion | flops 31457280 | bytes 10584064 | tf_op jit(solution)/shard_map/bsij,bsj->bi/dot_general | solution.py:58
  281.4 4.9 %all_to_all.104 = f32[2,1,3]{2,1,0:T(1,128)S(1)} all-to-all(f32[2,1,3]{2,1,0:T(1,128)S(1)} %broadcast_in_dim.87), channel_id=1, replica_groups=mesh['dom_0'=4,'dom_1'=4,'dom_2'=4,'dom_3'=2] {'dom_3'}, dimensions={0} | all-to-all | bytes 48 | tf_op jit(solution)/shard_map/all_to_all | solution.py:22
  286.3 12.4 %all_to_all.105 = f32[64,1,3]{2,1,0:T(1,128)S(1)} all-to-all(f32[64,1,3]{2,1,0:T(1,128)S(1)} %broadcast_in_dim.88), channel_id=1, replica_groups=mesh['dom_0'=4,'dom_1'=4,'dom_2'=4,'dom_3'=2] {'dom_0','dom_1','dom_2'}, dimensions={0} | all-to-all | bytes 1536 | tf_op jit(solution)/shard_map/all_to_all | solution.py:22
  299.7 2.1 collective-permute-start.24
  304.9 6.8 %collective-permute-done.27 = f32[16,128]{1,0:T(8,128)S(1)} collective-permute-done((f32[16,128]{1,0:T(8,128)S(1)}, f32[16,128]{1,0:T(8,128)S(1)}, u32[]{:S(2)}, u32[]{:S(2)}) %collective-permute-start.27) | collective-permute-done | bytes 8224 | tf_op jit(solution)/shard_map/ppermute | solution.py:17
  312.5 12.6 %fusion.24 = f32[32,1,128,1]{2,1,3,0:T(1,128)S(1)} fusion(f32[32,5,128,128]{3,2,1,0:T(8,128)} %param.58, f32[32,5,128,1]{2,1,0,3:T(8,128)S(1)} %multiply_bitcast_fusion.1), kind=kOutput, calls=%fused_computation.120 | convolution fusion | flops 31457280 | bytes 10584064 | tf_op jit(solution)/shard_map/bsij,bsj->bi/dot_general | solution.py:58
  327.6 4.8 %all_to_all.106 = f32[2,1,5]{2,1,0:T(1,128)S(1)} all-to-all(f32[2,1,5]{2,1,0:T(1,128)S(1)} %broadcast_in_dim.89), channel_id=1, replica_groups=mesh['dom_0'=4,'dom_1'=4,'dom_2'=4,'dom_3'=2] {'dom_3'}, dimensions={0} | all-to-all | bytes 80 | tf_op jit(solution)/shard_map/all_to_all | solution.py:22
  333.0 4.6 %all-to-all-start.13 = ((f32[64,1,5]{2,1,0:T(1,128)}), f32[64,1,5]{2,1,0:T(1,128)S(1)}, u32[]{:S(2)}, u32[]{:S(2)}) async-start(f32[64,1,5]{2,1,0:T(1,128)} %broadcast_in_dim.90), calls=%async_computation.13 | async-start | bytes 65536 | tf_op jit(solution)/shard_map/all_to_all | solution.py:22
  337.7 8.4 %all-to-all-done.13 = f32[64,1,5]{2,1,0:T(1,128)S(1)} async-done(((f32[64,1,5]{2,1,0:T(1,128)}), f32[64,1,5]{2,1,0:T(1,128)S(1)}, u32[]{:S(2)}, u32[]{:S(2)}) %all-to-all-start.13) | async-done | bytes 1312 | tf_op jit(solution)/shard_map/all_to_all | solution.py:22
  349.1 2.1 collective-permute-start.28
  355.0 6.9 %collective-permute-done.31 = f32[16,128]{1,0:T(8,128)S(1)} collective-permute-done((f32[16,128]{1,0:T(8,128)S(1)}, f32[16,128]{1,0:T(8,128)S(1)}, u32[]{:S(2)}, u32[]{:S(2)}) %collective-permute-start.31) | collective-permute-done | bytes 8224 | tf_op jit(solution)/shard_map/ppermute | solution.py:17
  362.7 12.6 %fusion.22 = f32[32,1,128,1]{2,1,3,0:T(1,128)S(1)} fusion(f32[32,5,128,128]{3,2,1,0:T(8,128)} %param.58, f32[32,5,128,1]{2,1,0,3:T(8,128)S(1)} %multiply_bitcast_fusion), kind=kOutput, calls=%fused_computation.118 | convolution fusion | flops 31457280 | bytes 10584064 | tf_op jit(solution)/shard_map/bsij,bsj->bi/dot_general | solution.py:58
  377.9 4.7 %all_to_all.107 = f32[2,1,5]{2,1,0:T(1,128)S(1)} all-to-all(f32[2,1,5]{2,1,0:T(1,128)S(1)} %broadcast_in_dim.91), channel_id=1, replica_groups=mesh['dom_0'=4,'dom_1'=4,'dom_2'=4,'dom_3'=2] {'dom_3'}, dimensions={0} | all-to-all | bytes 80 | tf_op jit(solution)/shard_map/all_to_all | solution.py:22
  383.3 4.6 %all-to-all-start.15 = ((f32[64,1,5]{2,1,0:T(1,128)}), f32[64,1,5]{2,1,0:T(1,128)S(1)}, u32[]{:S(2)}, u32[]{:S(2)}) async-start(f32[64,1,5]{2,1,0:T(1,128)} %broadcast_in_dim.92), calls=%async_computation.15 | async-start | bytes 65536 | tf_op jit(solution)/shard_map/all_to_all | solution.py:22
  388.5 7.8 %all-to-all-done.15 = f32[64,1,5]{2,1,0:T(1,128)S(1)} async-done(((f32[64,1,5]{2,1,0:T(1,128)}), f32[64,1,5]{2,1,0:T(1,128)S(1)}, u32[]{:S(2)}, u32[]{:S(2)}) %all-to-all-start.15) | async-done | bytes 1312 | tf_op jit(solution)/shard_map/all_to_all | solution.py:22
  398.7 2.5 fusion.81
  401.2 2.0 scatter.116
  (274 shorter events, 76.1 us)
Async XLA Ops:
  0.0 34.5 %copy-start = (f32[32,128]{1,0:T(8,128)S(1)}, f32[32,128]{1,0:T(8,128)}, u32[]{:S(2)}) copy-start(f32[32,128]{1,0:T(8,128)} %param.55) | copy-start | bytes 49156
  0.0 34.5 %copy-start.1 = (f32[32,128]{1,0:T(8,128)S(1)}, f32[32,128]{1,0:T(8,128)}, u32[]{:S(2)}) copy-start(f32[32,128]{1,0:T(8,128)} %param.56) | copy-start | bytes 49156
  2.1 13.4 %collective-permute-start = (f32[16,128]{1,0:T(8,128)S(1)}, f32[16,128]{1,0:T(8,128)S(1)}, u32[]{:S(2)}, u32[]{:S(2)}) collective-permute-start(f32[16,128]{1,0:T(8,128)S(1)} %get-tuple-element.356), channel_id=1, source_target_pairs={{0,126},{1,127},{2,0},{3,1},{4,2},{5,3},{6,4},{7,5},{8,6},{9,7},{1... | collective-permute-start | bytes 24584 | tf_op jit(solution)/shard_map/ppermute | solution.py:17
  11.4 4.1 %collective-permute-start.1 = (f32[16,128]{1,0:T(8,128)S(1)}, f32[16,128]{1,0:T(8,128)S(1)}, u32[]{:S(2)}, u32[]{:S(2)}) collective-permute-start(f32[16,128]{1,0:T(8,128)S(1)} %get-tuple-element.355), channel_id=1, source_target_pairs={{0,127},{1,0},{2,1},{3,2},{4,3},{5,4},{6,5},{7,6},{8,7},{9,8},{10,... | collective-permute-start | bytes 24584 | tf_op jit(solution)/shard_map/ppermute | solution.py:17
  12.4 3.2 collective-permute-start.2
  13.2 7.9 %collective-permute-start.3 = (f32[16,128]{1,0:T(8,128)S(1)}, f32[16,128]{1,0:T(8,128)S(1)}, u32[]{:S(2)}, u32[]{:S(2)}) collective-permute-start(f32[16,128]{1,0:T(8,128)S(1)} %get-tuple-element.353), channel_id=1, source_target_pairs={{0,2},{1,3},{2,4},{3,5},{4,6},{5,7},{6,8},{7,9},{8,10},{9,11},{10,... | collective-permute-start | bytes 24584 | tf_op jit(solution)/shard_map/ppermute | solution.py:17
  55.5 4.1 %collective-permute-start.4 = (f32[16,128]{1,0:T(8,128)S(1)}, f32[16,128]{1,0:T(8,128)S(1)}, u32[]{:S(2)}, u32[]{:S(2)}) collective-permute-start(f32[16,128]{1,0:T(8,128)S(1)} %get-tuple-element.352), channel_id=1, source_target_pairs={{0,126},{1,127},{2,0},{3,1},{4,2},{5,3},{6,4},{7,5},{8,6},{9,7},{1... | collective-permute-start | bytes 24584 | tf_op jit(solution)/shard_map/ppermute | solution.py:17
  57.7 3.1 collective-permute-start.5
  59.4 1.3 collective-permute-start.6
  59.4 8.1 %collective-permute-start.7 = (f32[16,128]{1,0:T(8,128)S(1)}, f32[16,128]{1,0:T(8,128)S(1)}, u32[]{:S(2)}, u32[]{:S(2)}) collective-permute-start(f32[16,128]{1,0:T(8,128)S(1)} %get-tuple-element.349), channel_id=1, source_target_pairs={{0,2},{1,3},{2,4},{3,5},{4,6},{5,7},{6,8},{7,9},{8,10},{9,11},{10,... | collective-permute-start | bytes 24584 | tf_op jit(solution)/shard_map/ppermute | solution.py:17
  99.7 3.9 collective-permute-start.8
  101.8 3.1 collective-permute-start.9
  103.6 1.3 collective-permute-start.10
  103.6 8.1 %collective-permute-start.11 = (f32[16,128]{1,0:T(8,128)S(1)}, f32[16,128]{1,0:T(8,128)S(1)}, u32[]{:S(2)}, u32[]{:S(2)}) collective-permute-start(f32[16,128]{1,0:T(8,128)S(1)} %get-tuple-element.345), channel_id=1, source_target_pairs={{0,2},{1,3},{2,4},{3,5},{4,6},{5,7},{6,8},{7,9},{8,10},{9,11},{10,... | collective-permute-start | bytes 24584 | tf_op jit(solution)/shard_map/ppermute | solution.py:17
  133.5 13.1 %all-to-all-start.5 = ((f32[64,1,5]{2,1,0:T(1,128)}), f32[64,1,5]{2,1,0:T(1,128)S(1)}, u32[]{:S(2)}, u32[]{:S(2)}) async-start(f32[64,1,5]{2,1,0:T(1,128)} %broadcast_in_dim.40), calls=%async_computation.5 | async-start | bytes 65536 | tf_op jit(solution)/shard_map/all_to_all | solution.py:22
  149.6 4.7 %collective-permute-start.12 = (f32[16,128]{1,0:T(8,128)S(1)}, f32[16,128]{1,0:T(8,128)S(1)}, u32[]{:S(2)}, u32[]{:S(2)}) collective-permute-start(f32[16,128]{1,0:T(8,128)S(1)} %get-tuple-element.344), channel_id=1, source_target_pairs={{0,126},{1,127},{2,0},{3,1},{4,2},{5,3},{6,4},{7,5},{8,6},{9,7},{1... | collective-permute-start | bytes 24584 | tf_op jit(solution)/shard_map/ppermute | solution.py:17
  152.4 3.1 collective-permute-start.13
  154.2 1.3 collective-permute-start.14
  154.2 8.2 %collective-permute-start.15 = (f32[16,128]{1,0:T(8,128)S(1)}, f32[16,128]{1,0:T(8,128)S(1)}, u32[]{:S(2)}, u32[]{:S(2)}) collective-permute-start(f32[16,128]{1,0:T(8,128)S(1)} %get-tuple-element.341), channel_id=1, source_target_pairs={{0,2},{1,3},{2,4},{3,5},{4,6},{5,7},{6,8},{7,9},{8,10},{9,11},{10,... | collective-permute-start | bytes 24584 | tf_op jit(solution)/shard_map/ppermute | solution.py:17
  183.7 13.1 %all-to-all-start.7 = ((f32[64,1,5]{2,1,0:T(1,128)}), f32[64,1,5]{2,1,0:T(1,128)S(1)}, u32[]{:S(2)}, u32[]{:S(2)}) async-start(f32[64,1,5]{2,1,0:T(1,128)} %broadcast_in_dim.84), calls=%async_computation.7 | async-start | bytes 65536 | tf_op jit(solution)/shard_map/all_to_all | solution.py:22
  207.9 4.1 collective-permute-start.16
  210.1 3.1 collective-permute-start.17
  211.8 1.3 collective-permute-start.18
  211.8 8.1 %collective-permute-start.19 = (f32[16,128]{1,0:T(8,128)S(1)}, f32[16,128]{1,0:T(8,128)S(1)}, u32[]{:S(2)}, u32[]{:S(2)}) collective-permute-start(f32[16,128]{1,0:T(8,128)S(1)} %get-tuple-element.337), channel_id=1, source_target_pairs={{0,2},{1,3},{2,4},{3,5},{4,6},{5,7},{6,8},{7,9},{8,10},{9,11},{10,... | collective-permute-start | bytes 24584 | tf_op jit(solution)/shard_map/ppermute | solution.py:17
  255.5 3.9 collective-permute-start.20
  257.6 3.1 collective-permute-start.21
  259.4 1.3 collective-permute-start.22
  259.4 8.1 %collective-permute-start.23 = (f32[16,128]{1,0:T(8,128)S(1)}, f32[16,128]{1,0:T(8,128)S(1)}, u32[]{:S(2)}, u32[]{:S(2)}) collective-permute-start(f32[16,128]{1,0:T(8,128)S(1)} %get-tuple-element.333), channel_id=1, source_target_pairs={{0,2},{1,3},{2,4},{3,5},{4,6},{5,7},{6,8},{7,9},{8,10},{9,11},{10,... | collective-permute-start | bytes 24584 | tf_op jit(solution)/shard_map/ppermute | solution.py:17
  299.7 3.9 collective-permute-start.24
  301.8 3.1 collective-permute-start.25
  303.6 1.3 collective-permute-start.26
  303.6 8.1 %collective-permute-start.27 = (f32[16,128]{1,0:T(8,128)S(1)}, f32[16,128]{1,0:T(8,128)S(1)}, u32[]{:S(2)}, u32[]{:S(2)}) collective-permute-start(f32[16,128]{1,0:T(8,128)S(1)} %get-tuple-element.329), channel_id=1, source_target_pairs={{0,2},{1,3},{2,4},{3,5},{4,6},{5,7},{6,8},{7,9},{8,10},{9,11},{10,... | collective-permute-start | bytes 24584 | tf_op jit(solution)/shard_map/ppermute | solution.py:17
  333.0 13.1 %all-to-all-start.13 = ((f32[64,1,5]{2,1,0:T(1,128)}), f32[64,1,5]{2,1,0:T(1,128)S(1)}, u32[]{:S(2)}, u32[]{:S(2)}) async-start(f32[64,1,5]{2,1,0:T(1,128)} %broadcast_in_dim.90), calls=%async_computation.13 | async-start | bytes 65536 | tf_op jit(solution)/shard_map/all_to_all | solution.py:22
  349.1 5.0 %collective-permute-start.28 = (f32[16,128]{1,0:T(8,128)S(1)}, f32[16,128]{1,0:T(8,128)S(1)}, u32[]{:S(2)}, u32[]{:S(2)}) collective-permute-start(f32[16,128]{1,0:T(8,128)S(1)} %get-tuple-element.328), channel_id=1, source_target_pairs={{0,126},{1,127},{2,0},{3,1},{4,2},{5,3},{6,4},{7,5},{8,6},{9,7},{1... | collective-permute-start | bytes 24584 | tf_op jit(solution)/shard_map/ppermute | solution.py:17
  351.9 3.1 collective-permute-start.29
  353.7 1.3 collective-permute-start.30
  353.7 8.2 %collective-permute-start.31 = (f32[16,128]{1,0:T(8,128)S(1)}, f32[16,128]{1,0:T(8,128)S(1)}, u32[]{:S(2)}, u32[]{:S(2)}) collective-permute-start(f32[16,128]{1,0:T(8,128)S(1)} %get-tuple-element.325), channel_id=1, source_target_pairs={{0,2},{1,3},{2,4},{3,5},{4,6},{5,7},{6,8},{7,9},{8,10},{9,11},{10,... | collective-permute-start | bytes 24584 | tf_op jit(solution)/shard_map/ppermute | solution.py:17
  383.3 13.1 %all-to-all-start.15 = ((f32[64,1,5]{2,1,0:T(1,128)}), f32[64,1,5]{2,1,0:T(1,128)S(1)}, u32[]{:S(2)}, u32[]{:S(2)}) async-start(f32[64,1,5]{2,1,0:T(1,128)} %broadcast_in_dim.92), calls=%async_computation.15 | async-start | bytes 65536 | tf_op jit(solution)/shard_map/all_to_all | solution.py:22
where the time goes:
time: 416 us; the launch traced here: 408 us
  matrix products  112 us (27%)
  waiting for transfers between devices  90.8 us (22%)
  blocking collectives  87.8 us (21%)
  starting transfers between devices  57.3 us (14%)
  other arithmetic  26.1 us (6%)
  local copies, waits for them, and re-layouts  25.7 us (6%)
  between operations  8.62 us (2%)
    dot_general x8, matrix products, product(): jnp.einsum('bsij,bsj->bi', block_values, gathered, precision=lax.Precisio...  101 us
    all_to_all x12, blocking collectives, from_everyone(): return lax.all_to_all(copies, axis, split_axis=0, concat_axis=0, tiled=True)  87.8 us
    ppermute x32, waiting for transfers between devices, passed_along(): lax.ppermute(value, axis, [(i, (i + by) % length) for i in range(length)])  61.4 us
    ppermute x32, starting transfers between devices, passed_along(): lax.ppermute(value, axis, [(i, (i + by) % length) for i in range(length)])  38.9 us
    all_to_all x4, waiting for transfers between devices, from_everyone(): return lax.all_to_all(copies, axis, split_axis=0, concat_axis=0, tiled=True)  29.3 us
    all_to_all x4, starting transfers between devices, from_everyone(): return lax.all_to_all(copies, axis, split_axis=0, concat_axis=0, tiled=True)  18.5 us
    another operation x12, other arithmetic  9.37 us
  transfers between devices with their start and end apart: 36, of which 19 were waited for; matrix products, arithmetic and copies ran while one was open for 2% of the time, Pallas kernels for 0%

commit v1 on v0

v1 whole, which is shorter than its diff:
```python
import jax
import jax.numpy as jnp
from jax import lax
from jax.experimental import pallas as pl
from jax.experimental.pallas import tpu as pltpu
from jax.sharding import PartitionSpec as P

BLK = 128
BDEV = 32
NNZB = 5
GMAX = 16
OFFSETS = (-2, -1, 1, 2)
ORDER = (0, 3, 1, 2)
EPS = 1e-6
SHIFT = 8.0
SCALE = 0.25
ROUNDS = 7
GROUP = 8
CHUNK = 4
ZERO_ROW = BDEV + 4 * GMAX
XROWS = ZERO_ROW + 8
PAIRS = ((0, 0), (0, 1), (0, 2), (1, 1), (1, 2), (2, 2), (0, 3), (1, 3), (2, 3))
MESH = pl.DeviceIdType.MESH


def arnoldi_weights(gram, substep):
    G = {}
    for (i, j), g in gram.items():
        G[i, j] = g
        G[j, i] = g
    zero = jnp.zeros_like(substep)
    magnitude = jnp.sqrt(G[0, 0] + EPS)
    vectors = [[1.0 / magnitude]]
    H = [[None] * 3 for _ in range(3)]
    for col in range(3):
        v = vectors[col]
        n = len(v)
        mapped = [None] * (n + 1)
        for k in range(n + 1):
            term = None
            if k > 0:
                term = v[k - 1] * (1.0 / SCALE)
            if k < n:
                low = v[k] * SHIFT
                term = -low if term is None else term - low
            mapped[k] = term
        image = []
        for i in range(n):
            total = G[i, 0] * mapped[0]
            for k in range(1, n + 1):
                total = total + G[i, k] * mapped[k]
            image.append(total)
        projections = []
        for vec in vectors:
            total = vec[0] * image[0]
            for k in range(1, len(vec)):
                total = total + vec[k] * image[k]
            projections.append(total)
        for k, p in enumerate(projections):
            H[k][col] = p
        if col < 2:
            rest = list(mapped)
            for p, vec in zip(projections, vectors):
                for k in range(len(vec)):
                    rest[k] = rest[k] - p * vec[k]
            square = None
            for i in range(n + 1):
                total = G[i, 0] * rest[0]
                for k in range(1, n + 1):
                    total = total + G[i, k] * rest[k]
                total = total * rest[i]
                square = total if square is None else square + total
            length = jnp.sqrt(square + EPS)
            H[col + 1][col] = length
            inverse = 1.0 / length
            vectors.append([r * inverse for r in rest])
    small = substep * (1.0 / 64.0)
    A = [[None if H[i][j] is None else H[i][j] * small for j in range(3)] for i in range(3)]
    one = jnp.ones_like(substep)
    Pm = [[one if i == j else zero for j in range(3)] for i in range(3)]
    q = [zero] * 3
    for degree in range(12, 0, -1):
        inv = 1.0 / degree
        newP = [[None] * 3 for _ in range(3)]
        newq = [None] * 3
        for i in range(3):
            ks = [k for k in range(3) if A[i][k] is not None]
            for j in range(3):
                total = A[i][ks[0]] * Pm[ks[0]][j]
                for k in ks[1:]:
                    total = total + A[i][k] * Pm[k][j]
                total = total * inv
                newP[i][j] = total + 1.0 if i == j else total
            total = A[i][ks[0]] * q[ks[0]]
            for k in ks[1:]:
                total = total + A[i][k] * q[k]
            if i == 0:
                total = total + (1.0 / 64.0)
            newq[i] = total * inv
        Pm, q = newP, newq
    for _ in range(6):
        newP = [[Pm[i][0] * Pm[0][j] + Pm[i][1] * Pm[1][j] + Pm[i][2] * Pm[2][j] for j in range(3)] for i in range(3)]
        q = [Pm[i][0] * q[0] + Pm[i][1] * q[1] + Pm[i][2] * q[2] + q[i] for i in range(3)]
        Pm = newP
    out = []
    for k in range(3):
        total = None
        for col in range(k, 3):
            term = q[col] * vectors[col][k]
            total = term if total is None else total + term
        out.append(total * (substep * magnitude))
    return out


def kernel(ndev, conc_hbm, rate_hbm, step_hbm, blocks_hbm, cols_hbm, lens_hbm, lists_hbm, out_hbm, *scratch):
    (conc, rate, slope8, blocks, ys, sends, gram_row, arrivals, result, step_s, cols_s, lens_s, lists_s, index_s) = scratch[:14]
    xs = scratch[14 : 14 + ROUNDS]
    in_sems, block_sems, send_sems, recv_sems, ar_send, ar_recv, out_sem = scratch[14 + ROUNDS :]
    me = lax.axis_index("dom")

    small = [
        pltpu.make_async_copy(lists_hbm, lists_s, in_sems.at[0]),
        pltpu.make_async_copy(conc_hbm, conc, in_sems.at[1]),
        pltpu.make_async_copy(cols_hbm, cols_s, in_sems.at[2]),
        pltpu.make_async_copy(lens_hbm, lens_s, in_sems.at[3]),
        pltpu.make_async_copy(rate_hbm, rate, in_sems.at[4]),
        pltpu.make_async_copy(step_hbm, step_s, in_sems.at[5]),
    ]
    for copy in small:
        copy.start()
    chunks = []
    for c in range(BDEV // CHUNK):
        part = pl.ds(c * CHUNK, CHUNK)
        chunks.append(pltpu.make_async_copy(blocks_hbm.at[part], blocks.at[part], block_sems.at[c]))
        chunks[-1].start()

    barrier = pltpu.get_barrier_semaphore()

    def greet(k, carry):
        pl.semaphore_signal(barrier, inc=1, device_id=(lax.rem(me + k, ndev),), device_id_type=MESH)
        return carry

    lax.fori_loop(1, ndev, greet, 0)

    for x in xs:
        x[pl.ds(ZERO_ROW, 8), :] = jnp.zeros((8, BLK), jnp.float32)
    for copy in small:
        copy.wait()

    def remap(b, carry):
        length = lens_s[b]
        for t in range(NNZB):
            index_s[b * NNZB + t] = jnp.where(t < length, cols_s[b, t], ZERO_ROW)
        return carry

    lax.fori_loop(0, BDEV, remap, 0)

    def packet(r, q):
        o = OFFSETS[q]
        return pltpu.make_async_remote_copy(
            src_ref=sends.at[r, q],
            dst_ref=xs[r].at[pl.ds(BDEV + q * GMAX, GMAX), :],
            send_sem=send_sems.at[r, q],
            recv_sem=recv_sems.at[r, q],
            device_id=(lax.rem(me + (o + ndev), ndev),),
            device_id_type=MESH,
        )

    def pack(r, source):
        for q in ORDER:
            for g in range(GMAX):
                sends[r, q, pl.ds(g, 1), :] = source[pl.ds(lists_s[0, q, g], 1), :]
            if r > 0:
                packet(r, q).start()

    def await_ghosts(r):
        for q in ORDER:
            packet(r, q).wait_recv()

    def product(r, finish):
        x = xs[r]

        def group(i, carry):
            for s in range(GROUP):
                b = i * GROUP + s
                total = None
                for t in range(NNZB):
                    row = x[pl.ds(index_s[b * NNZB + t], 8, stride=0), :]
                    term = blocks[b, t].reshape(16, 8, BLK) * row[None]
                    total = term if total is None else total + term
                flipped = total.reshape(BLK, BLK).T
                finish(b, jnp.sum(flipped, axis=0, keepdims=True))
            return carry

        if r == 0:
            for i in range(BDEV // GROUP):
                for c in range(i * GROUP // CHUNK, (i + 1) * GROUP // CHUNK):
                    chunks[c].wait()
                group(i, 0)
        else:
            lax.fori_loop(0, BDEV // GROUP, group, 0)

    pack(0, conc)
    xs[0][pl.ds(0, BDEV), :] = conc[...]
    slope8[...] = rate[...] * (1.0 - 2.0 * conc[...]) + SHIFT
    pl.semaphore_wait(barrier, ndev - 1)
    for q in ORDER:
        packet(0, q).start()
    await_ghosts(0)

    def first(b, row):
        c = conc[pl.ds(b, 1), :]
        ys[0, pl.ds(b, 1), :] = rate[pl.ds(b, 1), :] * c * (1.0 - c) - row

    product(0, first)

    def broadcast_gram(slot, products):
        rows = [jnp.sum(p, axis=0, keepdims=True) for p in products]
        rows = rows + [jnp.zeros((BLK - len(rows), BLK), jnp.float32)]
        gram_row[slot] = jnp.sum(jnp.concatenate(rows, axis=0).T, axis=0, keepdims=True)

        def send(k, carry):
            pltpu.make_async_remote_copy(
                src_ref=gram_row.at[slot],
                dst_ref=arrivals.at[slot, me],
                send_sem=ar_send.at[slot],
                recv_sem=ar_recv.at[slot],
                device_id=(lax.rem(me + k, ndev),),
                device_id_type=MESH,
            ).start()
            return carry

        lax.fori_loop(1, ndev, send, 0)

    def collect_gram(slot):
        whole = arrivals.at[slot, pl.ds(0, ndev - 1)]
        pltpu.make_async_copy(whole, whole, ar_recv.at[slot]).wait()
        arrivals[slot, me] = gram_row[slot]
        total = jnp.sum(arrivals[slot], axis=0)
        return {
            pair: jnp.broadcast_to(total[:, e : e + 1], (1, BLK)) for e, pair in enumerate(PAIRS)
        }

    substep = jnp.full((1, BLK), step_s[0] * 0.5, jnp.float32)
    us = None
    for r in range(1, ROUNDS):
        pack(r, ys.at[r - 1])
        xs[r][pl.ds(0, BDEV), :] = ys[r - 1]
        if r == 4:
            w = [ys[k] for k in range(4)]
            broadcast_gram(0, [w[i] * w[j] for i, j in PAIRS])
        if r == ROUNDS - 1:
            w = [ys[k] for k in range(6)]
            first_weights = arnoldi_weights(collect_gram(0), substep)
            d = [None] * 4
            for k in range(4):
                term = None
                if k > 0:
                    term = first_weights[k - 1] * (1.0 / SCALE)
                if k < 3:
                    low = first_weights[k] * SHIFT
                    term = -low if term is None else term - low
                d[k] = term
            d[0] = d[0] + 1.0
            us = [d[0] * w[k] + d[1] * w[k + 1] + d[2] * w[k + 2] + d[3] * w[k + 3] for k in range(3)]
            tail = d[0] * w[3] + d[1] * w[4] + d[2] * w[5]
            partial = [us[i] * us[j] for i, j in PAIRS[:6]]
            base = (
                conc[...] + first_weights[0] * w[0] + first_weights[1] * w[1] + first_weights[2] * w[2]
            )
        await_ghosts(r)

        def later(b, row, r=r):
            ys[r, pl.ds(b, 1), :] = (
                slope8[pl.ds(b, 1), :] * ys[r - 1, pl.ds(b, 1), :] - row
            ) * SCALE

        product(r, later)
    last = tail + d[3] * ys[ROUNDS - 1]
    broadcast_gram(1, partial + [us[i] * last for i in range(3)])
    second = arnoldi_weights(collect_gram(1), substep)
    result[...] = base + second[0] * us[0] + second[1] * us[1] + second[2] * us[2]
    out = pltpu.make_async_copy(result, out_hbm, out_sem)
    out.start()
    for r in range(ROUNDS):
        for q in range(4):
            packet(r, q).wait_send()
    for slot in range(2):
        whole = arrivals.at[slot, pl.ds(0, ndev - 1)]
        pltpu.make_async_copy(whole, whole, ar_send.at[slot]).wait()
    out.wait()


def solution(mesh):
    ndev = mesh.shape["dom"]

    def step(conc, rate, size, blocks, cols, lens, lists):
        f32, i32 = jnp.float32, jnp.int32
        return pl.pallas_call(
            lambda *refs: kernel(ndev, *refs),
            out_shape=jax.ShapeDtypeStruct((BDEV, BLK), f32),
            in_specs=[pl.BlockSpec(memory_space=pl.ANY)] * 7,
            out_specs=pl.BlockSpec(memory_space=pl.ANY),
            scratch_shapes=[
                pltpu.VMEM((BDEV, BLK), f32),
                pltpu.VMEM((BDEV, BLK), f32),
                pltpu.VMEM((BDEV, BLK), f32),
                pltpu.VMEM((BDEV, NNZB, BLK, BLK), f32),
                pltpu.VMEM((ROUNDS, BDEV, BLK), f32),
                pltpu.VMEM((ROUNDS, 4, GMAX, BLK), f32),
                pltpu.VMEM((2, 1, BLK), f32),
                pltpu.VMEM((2, ndev, 1, BLK), f32),
                pltpu.VMEM((BDEV, BLK), f32),
                pltpu.SMEM((1,), f32),
                pltpu.SMEM((BDEV, NNZB), i32),
                pltpu.SMEM((BDEV,), i32),
                pltpu.SMEM((1, 4, GMAX), i32),
                pltpu.SMEM((BDEV * NNZB,), i32),
            ]
            + [pltpu.VMEM((XROWS, BLK), f32)] * ROUNDS
            + [
                pltpu.SemaphoreType.DMA((6,)),
                pltpu.SemaphoreType.DMA((BDEV // CHUNK,)),
                pltpu.SemaphoreType.DMA((ROUNDS, 4)),
                pltpu.SemaphoreType.DMA((ROUNDS, 4)),
                pltpu.SemaphoreType.DMA((2,)),
                pltpu.SemaphoreType.DMA((2,)),
                pltpu.SemaphoreType.DMA,
            ],
            compiler_params=pltpu.CompilerParams(collective_id=0, has_side_effects=True),
            name="rosenbrock",
        )(conc, rate, size, blocks, cols, lens, lists)

    dom = "dom"
    return jax.shard_map(
        step,
        mesh=mesh,
        in_specs=(P(dom), P(dom), P(), P(dom), P(dom), P(dom), P(dom)),
        out_specs=P(dom),
        check_vma=False,
    )
```

time: 416 us -> 66.1 us (0.16); the launches traced: 408 us -> 65.9 us
  matrix products: 112 us -> 0 us
  waiting for transfers between devices: 90.8 us -> 0 us
  blocking collectives: 87.8 us -> 0 us
  Pallas kernels: 0 us -> 62.5 us
  starting transfers between devices: 57.3 us -> 0 us
  other arithmetic: 26.1 us -> 0 us
  local copies, waits for them, and re-layouts: 25.7 us -> 2.7 us
  between operations: 8.62 us -> 0.66 us
    dot_general x56 -> x0, matrix products: 112 us -> none  [the longest x8 101 us: product(): jnp.einsum('bsij,bsj->bi', block_values, gathered, precision=lax.Precisio...]
    all_to_all x12 -> x0, blocking collectives: 87.8 us -> none  [from_everyone(): return lax.all_to_all(copies, axis, split_axis=0, concat_axis=0, tiled=True)]
    pallas_call x0 -> x1, Pallas kernels: none -> 62.5 us  [step(): pl.pallas_call(lambda *refs: kernel(ndev, *refs), out_shape=jax.ShapeDtyp...]
    ppermute x32 -> x0, waiting for transfers between devices: 61.4 us -> none  [passed_along(): lax.ppermute(value, axis, [(i, (i + by) % length) for i in range(length)])]
    ppermute x32 -> x0, starting transfers between devices: 38.9 us -> none  [passed_along(): lax.ppermute(value, axis, [(i, (i + by) % length) for i in range(length)])]
    all_to_all x4 -> x0, waiting for transfers between devices: 29.3 us -> none  [from_everyone(): return lax.all_to_all(copies, axis, split_axis=0, concat_axis=0, tiled=True)]
    all_to_all x4 -> x0, starting transfers between devices: 18.5 us -> none  [from_everyone(): return lax.all_to_all(copies, axis, split_axis=0, concat_axis=0, tiled=True)]
    gather x24 -> x0, local copies, waits for them, and re-layouts: 11 us -> none  [the longest x16 5.5 us: product(): gathered = extended[block_columns] * active[:, :, None]]
  transfers between devices with their start and end apart: 36 -> 0, of which waited for: 19 -> 0; matrix products, arithmetic and copies ran while one was open for 2% -> 0% of each run, Pallas kernels for 0% -> 0%
where the time goes in v1:
time: 66.1 us; the launch traced here: 65.9 us
  Pallas kernels  62.5 us (95%)
  local copies, waits for them, and re-layouts  2.7 us (4%)
    pallas_call x1, Pallas kernels, step(): pl.pallas_call(lambda *refs: kernel(ndev, *refs), out_shape=jax.ShapeDtyp...  62.5 us
    unnamed x2, local copies, waits for them, and re-layouts  2.7 us

profile of v1, /device:TPU:1, one launch (start us, length us, event | category | flops | bytes accessed | tf_op | source)
XLA Modules:
  0.0 65.9 jit_solution(8372946972796873295)
XLA Ops:
  0.7 1.4 %copy.8.refs_4_ = s32[32,5]{1,0:T(8,128)} copy(s32[32,5]{0,1:T(8,128)} %param.11) | data formatting | bytes 1280 | tf_op args[4]
  2.0 62.5 %rosenbrock.1 = f32[32,128]{1,0:T(8,128)} custom-call(f32[32,128]{1,0:T(8,128)} %refs_0_.1, f32[32,128]{1,0:T(8,128)} %refs_1_.1, f32[1]{0:T(128)S(6)} %copy.10.refs_2_, f32[32,5,128,128]{3,2,1,0:T(8,128)} %refs_3_.1, s32[32,5]{1,0:T(8,128)} %copy.8.refs_4_, s32[32]{0:T(128)} %refs_5_.1, s32[1,4,16]{2,1,0:T(4,128)} %refs_6_.1), custom_call_target="tpu_custom_call" | custom-call | tf_op jit(solution)/shard_map/rosenbrock/pallas_call | solution.py:299
  64.6 1.3 %copy.11 = f32[32,128]{1,0:T(8,128)} copy(f32[32,128]{1,0:T(8,128)} %rosenbrock.1) | data formatting | bytes 32768

commit v2 on v1

--- a/solution.py
+++ b/solution.py
@@ -112,11 +112,40 @@
     return out
 
 
-def kernel(ndev, conc_hbm, rate_hbm, step_hbm, blocks_hbm, cols_hbm, lens_hbm, lists_hbm, out_hbm, *scratch):
-    (conc, rate, slope8, blocks, ys, sends, gram_row, arrivals, result, step_s, cols_s, lens_s, lists_s, index_s) = scratch[:14]
+def far_first():
+    steps = (0, 1, 2, 1)
+    every = [(y, z, x, c) for y in range(4) for z in range(4) for x in range(4) for c in range(2)]
+    every.remove((0, 0, 0, 0))
+    return sorted(every, key=lambda o: (-(steps[o[0]] + steps[o[1]] + steps[o[2]]), o))
+
+
+def kernel(ndev, conc_hbm, rate_hbm, step_hbm, blocks_hbm, cols_hbm, lens_hbm, lists_hbm, result, *scratch):
+    (conc, rate, slope8, fixed, blocks, ys, sends, gram_row, arrivals, step_s, cols_s, lens_s, lists_s, index_s) = scratch[:14]
     xs = scratch[14 : 14 + ROUNDS]
-    in_sems, block_sems, send_sems, recv_sems, ar_send, ar_recv, out_sem = scratch[14 + ROUNDS :]
+    in_sems, block_sems, send_sems, recv_sems, ar_send, ar_recv, known_z, known_y = scratch[14 + ROUNDS :]
     me = lax.axis_index("dom")
+
+    def near(o):
+        return lax.rem(me + (o + ndev), ndev)
+
+    my_core, my_x = lax.rem(me, 2), lax.rem(me // 2, 4)
+    my_z, my_y = lax.rem(me // 8, 4), me // 32
+    at_y = [lax.rem(my_y + d, 4) * 32 for d in range(4)]
+    at_z = [lax.rem(my_z + d, 4) * 8 for d in range(4)]
+    at_x = [lax.rem(my_x + d, 4) * 2 for d in range(4)]
+    at_core = [my_core, 1 - my_core]
+
+    def at(o):
+        return at_y[o[0]] + at_z[o[1]] + at_x[o[2]] + at_core[o[3]]
+
+    row_line = [(0, 0, x, c) for x in range(4) for c in range(2) if (x, c) != (0, 0)]
+    z_line = [(0, d, 0, 0) for d in (1, 2, 3)]
+    y_line = [(d, 0, 0, 0) for d in (1, 2, 3)]
+
+    barrier = pltpu.get_barrier_semaphore()
+    greeted = [near(OFFSETS[q]) for q in ORDER] + [at(o) for o in z_line + y_line + row_line]
+    for device in greeted:
+        pl.semaphore_signal(barrier, inc=1, device_id=(device,), device_id_type=MESH)
 
     small = [
         pltpu.make_async_copy(lists_hbm, lists_s, in_sems.at[0]),
@@ -134,35 +163,13 @@
         chunks.append(pltpu.make_async_copy(blocks_hbm.at[part], blocks.at[part], block_sems.at[c]))
         chunks[-1].start()
 
-    barrier = pltpu.get_barrier_semaphore()
-
-    def greet(k, carry):
-        pl.semaphore_signal(barrier, inc=1, device_id=(lax.rem(me + k, ndev),), device_id_type=MESH)
-        return carry
-
-    lax.fori_loop(1, ndev, greet, 0)
-
-    for x in xs:
-        x[pl.ds(ZERO_ROW, 8), :] = jnp.zeros((8, BLK), jnp.float32)
-    for copy in small:
-        copy.wait()
-
-    def remap(b, carry):
-        length = lens_s[b]
-        for t in range(NNZB):
-            index_s[b * NNZB + t] = jnp.where(t < length, cols_s[b, t], ZERO_ROW)
-        return carry
-
-    lax.fori_loop(0, BDEV, remap, 0)
-
     def packet(r, q):
-        o = OFFSETS[q]
         return pltpu.make_async_remote_copy(
             src_ref=sends.at[r, q],
             dst_ref=xs[r].at[pl.ds(BDEV + q * GMAX, GMAX), :],
             send_sem=send_sems.at[r, q],
             recv_sem=recv_sems.at[r, q],
-            device_id=(lax.rem(me + (o + ndev), ndev),),
+            device_id=(near(OFFSETS[q]),),
             device_id_type=MESH,
         )
 
@@ -177,60 +184,78 @@
         for q in ORDER:
             packet(r, q).wait_recv()
 
-    def product(r, finish):
-        x = xs[r]
+    def lane_sums(total):
+        return jnp.sum(total.T, axis=0, keepdims=True)
+
+    def own_part(r):
+        source = conc if r == 0 else ys.at[r - 1]
 
         def group(i, carry):
             for s in range(GROUP):
                 b = i * GROUP + s
-                total = None
-                for t in range(NNZB):
-                    row = x[pl.ds(index_s[b * NNZB + t], 8, stride=0), :]
-                    term = blocks[b, t].reshape(16, 8, BLK) * row[None]
-                    total = term if total is None else total + term
-                flipped = total.reshape(BLK, BLK).T
-                finish(b, jnp.sum(flipped, axis=0, keepdims=True))
+                mine = source[pl.ds(b, 1), :]
+                here = lane_sums(blocks[b, 0] * mine)
+                if r == 0:
+                    kept = rate[pl.ds(b, 1), :] * mine * (1.0 - mine)
+                else:
+                    kept = slope8[pl.ds(b, 1), :] * mine
+                fixed[pl.ds(b, 1), :] = kept - here
             return carry
 
-        if r == 0:
-            for i in range(BDEV // GROUP):
-                for c in range(i * GROUP // CHUNK, (i + 1) * GROUP // CHUNK):
-                    chunks[c].wait()
-                group(i, 0)
-        else:
-            lax.fori_loop(0, BDEV // GROUP, group, 0)
-
+        lax.fori_loop(0, BDEV // GROUP, group, 0)
+
+    def product(r):
+        x = xs[r]
+        for b in range(BDEV):
+            total = None
+            for t in range(1, NNZB):
+                row = x[pl.ds(index_s[b * NNZB + t], 8, stride=0), :]
+                term = blocks[b, t].reshape(16, 8, BLK) * row[None]
+                total = term if total is None else total + term
+            whole = fixed[pl.ds(b, 1), :] - lane_sums(total.reshape(BLK, BLK))
+            ys[r, pl.ds(b, 1), :] = whole if r == 0 else whole * SCALE
+
+    small[0].wait()
+    small[1].wait()
     pack(0, conc)
-    xs[0][pl.ds(0, BDEV), :] = conc[...]
-    slope8[...] = rate[...] * (1.0 - 2.0 * conc[...]) + SHIFT
-    pl.semaphore_wait(barrier, ndev - 1)
+    pl.semaphore_wait(barrier, len(greeted))
     for q in ORDER:
         packet(0, q).start()
+    for o in z_line:
+        pl.semaphore_signal(known_z, inc=1, device_id=(at(o),), device_id_type=MESH)
+    xs[0][pl.ds(0, BDEV), :] = conc[...]
+    for x in xs:
+        x[pl.ds(ZERO_ROW, 8), :] = jnp.zeros((8, BLK), jnp.float32)
+    for copy in small[2:]:
+        copy.wait()
+    slope8[...] = rate[...] * (1.0 - 2.0 * conc[...]) + SHIFT
+
+    def remap(b, carry):
+        length = lens_s[b]
+        for t in range(1, NNZB):
+            index_s[b * NNZB + t] = jnp.where(t < length, cols_s[t, b], ZERO_ROW)
+        return carry
+
+    lax.fori_loop(0, BDEV, remap, 0)
+    for chunk in chunks:
+        chunk.wait()
+    own_part(0)
     await_ghosts(0)
-
-    def first(b, row):
-        c = conc[pl.ds(b, 1), :]
-        ys[0, pl.ds(b, 1), :] = rate[pl.ds(b, 1), :] * c * (1.0 - c) - row
-
-    product(0, first)
+    product(0)
 
     def broadcast_gram(slot, products):
         rows = [jnp.sum(p, axis=0, keepdims=True) for p in products]
         rows = rows + [jnp.zeros((BLK - len(rows), BLK), jnp.float32)]
         gram_row[slot] = jnp.sum(jnp.concatenate(rows, axis=0).T, axis=0, keepdims=True)
-
-        def send(k, carry):
+        for o in far_first():
             pltpu.make_async_remote_copy(
                 src_ref=gram_row.at[slot],
                 dst_ref=arrivals.at[slot, me],
                 send_sem=ar_send.at[slot],
                 recv_sem=ar_recv.at[slot],
-                device_id=(lax.rem(me + k, ndev),),
+                device_id=(at(o),),
                 device_id_type=MESH,
             ).start()
-            return carry
-
-        lax.fori_loop(1, ndev, send, 0)
 
     def collect_gram(slot):
         whole = arrivals.at[slot, pl.ds(0, ndev - 1)]
@@ -246,7 +271,13 @@
     for r in range(1, ROUNDS):
         pack(r, ys.at[r - 1])
         xs[r][pl.ds(0, BDEV), :] = ys[r - 1]
+        if r == 1:
+            pl.semaphore_wait(known_z, 3)
+            for o in y_line:
+                pl.semaphore_signal(known_y, inc=1, device_id=(at(o),), device_id_type=MESH)
+        own_part(r)
         if r == 4:
+            pl.semaphore_wait(known_y, 3)
             w = [ys[k] for k in range(4)]
             broadcast_gram(0, [w[i] * w[j] for i, j in PAIRS])
         if r == ROUNDS - 1:
@@ -269,26 +300,17 @@
                 conc[...] + first_weights[0] * w[0] + first_weights[1] * w[1] + first_weights[2] * w[2]
             )
         await_ghosts(r)
-
-        def later(b, row, r=r):
-            ys[r, pl.ds(b, 1), :] = (
-                slope8[pl.ds(b, 1), :] * ys[r - 1, pl.ds(b, 1), :] - row
-            ) * SCALE
-
-        product(r, later)
+        product(r)
     last = tail + d[3] * ys[ROUNDS - 1]
     broadcast_gram(1, partial + [us[i] * last for i in range(3)])
     second = arnoldi_weights(collect_gram(1), substep)
     result[...] = base + second[0] * us[0] + second[1] * us[1] + second[2] * us[2]
-    out = pltpu.make_async_copy(result, out_hbm, out_sem)
-    out.start()
     for r in range(ROUNDS):
         for q in range(4):
             packet(r, q).wait_send()
     for slot in range(2):
         whole = arrivals.at[slot, pl.ds(0, ndev - 1)]
         pltpu.make_async_copy(whole, whole, ar_send.at[slot]).wait()
-    out.wait()
 
 
 def solution(mesh):
@@ -298,10 +320,11 @@
         f32, i32 = jnp.float32, jnp.int32
         return pl.pallas_call(
             lambda *refs: kernel(ndev, *refs),
-            out_shape=jax.ShapeDtypeStruct((BDEV, BLK), f32),
+            out_shape=pltpu.VMEM((BDEV, BLK), f32),
             in_specs=[pl.BlockSpec(memory_space=pl.ANY)] * 7,
-            out_specs=pl.BlockSpec(memory_space=pl.ANY),
+            out_specs=pl.BlockSpec(memory_space=pltpu.VMEM),
             scratch_shapes=[
+                pltpu.VMEM((BDEV, BLK), f32),
                 pltpu.VMEM((BDEV, BLK), f32),
                 pltpu.VMEM((BDEV, BLK), f32),
                 pltpu.VMEM((BDEV, BLK), f32),
@@ -310,9 +333,8 @@
                 pltpu.VMEM((ROUNDS, 4, GMAX, BLK), f32),
                 pltpu.VMEM((2, 1, BLK), f32),
                 pltpu.VMEM((2, ndev, 1, BLK), f32),
-                pltpu.VMEM((BDEV, BLK), f32),
                 pltpu.SMEM((1,), f32),
-                pltpu.SMEM((BDEV, NNZB), i32),
+                pltpu.SMEM((NNZB, BDEV), i32),
                 pltpu.SMEM((BDEV,), i32),
                 pltpu.SMEM((1, 4, GMAX), i32),
                 pltpu.SMEM((BDEV * NNZB,), i32),
@@ -325,11 +347,12 @@
                 pltpu.SemaphoreType.DMA((ROUNDS, 4)),
                 pltpu.SemaphoreType.DMA((2,)),
                 pltpu.SemaphoreType.DMA((2,)),
-                pltpu.SemaphoreType.DMA,
+                pltpu.SemaphoreType.REGULAR,
+                pltpu.SemaphoreType.REGULAR,
             ],
             compiler_params=pltpu.CompilerParams(collective_id=0, has_side_effects=True),
             name="rosenbrock",
-        )(conc, rate, size, blocks, cols, lens, lists)
+        )(conc, rate, size, blocks, cols.T, lens, lists)
 
     dom = "dom"
     return jax.shard_map(

time: 66.1 us -> 60.2 us (0.911)
  Pallas kernels: 62.5 us -> 58.8 us
  local copies, waits for them, and re-layouts: 2.7 us -> 0.61 us
    pallas_call x1, Pallas kernels: 62.5 us -> 58.8 us  [step(): pl.pallas_call(lambda *refs: kernel(ndev, *refs), out_shape=pltpu.VMEM((B...]
    unnamed x2 -> x1, local copies, waits for them, and re-layouts: 2.7 us -> 0.61 us
where the time goes in v2:
time: 60.2 us; the launch traced here: 60.1 us
  Pallas kernels  58.8 us (98%)
  between operations  0.66 us (1%)
  local copies, waits for them, and re-layouts  0.61 us (1%)
    pallas_call x1, Pallas kernels, step(): pl.pallas_call(lambda *refs: kernel(ndev, *refs), out_shape=pltpu.VMEM((B...  58.8 us

profile of v2, /device:TPU:1, one launch (start us, length us, event | category | flops | bytes accessed | tf_op | source)
XLA Modules:
  0.0 60.1 jit_solution(12055239557510404476)
XLA Ops:
  0.7 58.8 %rosenbrock.1 = f32[32,128]{1,0:T(8,128)S(1)} custom-call(f32[32,128]{1,0:T(8,128)} %refs_0_.1, f32[32,128]{1,0:T(8,128)} %refs_1_.1, f32[1]{0:T(128)S(6)} %copy.10.refs_2_, f32[32,5,128,128]{3,2,1,0:T(8,128)} %refs_3_.1, s32[5,32]{1,0:T(8,128)} %bitcast.1, s32[32]{0:T(128)} %refs_5_.1, s32[1,4,16]{2,1,0:T(4,128)} %refs_6_.1), custom_call_target="tpu_custom_call" | custom-call | tf_op jit(solution)/shard_map/rosenbrock/pallas_call | solution.py:321
  59.5 0.6 %copy.9 = f32[32,128]{1,0:T(8,128)} copy(f32[32,128]{1,0:T(8,128)S(1)} %rosenbrock.1) | data formatting | bytes 32768

commit v3 on v2

--- a/solution.py
+++ b/solution.py
@@ -112,17 +112,11 @@
     return out
 
 
-def far_first():
-    steps = (0, 1, 2, 1)
-    every = [(y, z, x, c) for y in range(4) for z in range(4) for x in range(4) for c in range(2)]
-    every.remove((0, 0, 0, 0))
-    return sorted(every, key=lambda o: (-(steps[o[0]] + steps[o[1]] + steps[o[2]]), o))
-
-
 def kernel(ndev, conc_hbm, rate_hbm, step_hbm, blocks_hbm, cols_hbm, lens_hbm, lists_hbm, result, *scratch):
-    (conc, rate, slope8, fixed, blocks, ys, sends, gram_row, arrivals, step_s, cols_s, lens_s, lists_s, index_s) = scratch[:14]
-    xs = scratch[14 : 14 + ROUNDS]
-    in_sems, block_sems, send_sems, recv_sems, ar_send, ar_recv, known_z, known_y = scratch[14 + ROUNDS :]
+    (conc_in, rate_in, conc, rate, slope8, fixed, blocks, ys, sends, gram_row, arrivals, ordered) = scratch[:12]
+    (step_s, cols_s, lens_s, lists_s, index_s, place_s, row_s, pick_s) = scratch[12:20]
+    xs = scratch[20 : 20 + ROUNDS]
+    in_sems, block_sems, send_sems, recv_sems, ar_send, ar_recv, known_z, known_y = scratch[20 + ROUNDS :]
     me = lax.axis_index("dom")
 
     def near(o):
@@ -134,6 +128,7 @@
     at_z = [lax.rem(my_z + d, 4) * 8 for d in range(4)]
     at_x = [lax.rem(my_x + d, 4) * 2 for d in range(4)]
     at_core = [my_core, 1 - my_core]
+    urgent = jnp.where(my_x < 2, 0, 3 - my_core)
 
     def at(o):
         return at_y[o[0]] + at_z[o[1]] + at_x[o[2]] + at_core[o[3]]
@@ -149,10 +144,10 @@
 
     small = [
         pltpu.make_async_copy(lists_hbm, lists_s, in_sems.at[0]),
-        pltpu.make_async_copy(conc_hbm, conc, in_sems.at[1]),
+        pltpu.make_async_copy(conc_hbm, conc_in, in_sems.at[1]),
         pltpu.make_async_copy(cols_hbm, cols_s, in_sems.at[2]),
         pltpu.make_async_copy(lens_hbm, lens_s, in_sems.at[3]),
-        pltpu.make_async_copy(rate_hbm, rate, in_sems.at[4]),
+        pltpu.make_async_copy(rate_hbm, rate_in, in_sems.at[4]),
         pltpu.make_async_copy(step_hbm, step_s, in_sems.at[5]),
     ]
     for copy in small:
@@ -163,26 +158,20 @@
         chunks.append(pltpu.make_async_copy(blocks_hbm.at[part], blocks.at[part], block_sems.at[c]))
         chunks[-1].start()
 
-    def packet(r, q):
+    def packet(r, q, source):
+        offset = jnp.where(q < 2, q - 2, q - 1)
         return pltpu.make_async_remote_copy(
-            src_ref=sends.at[r, q],
-            dst_ref=xs[r].at[pl.ds(BDEV + q * GMAX, GMAX), :],
+            src_ref=source,
+            dst_ref=xs[r].at[pl.ds(pl.multiple_of(BDEV + q * GMAX, 8), GMAX), :],
             send_sem=send_sems.at[r, q],
             recv_sem=recv_sems.at[r, q],
-            device_id=(near(OFFSETS[q]),),
+            device_id=(lax.rem(me + offset + ndev, ndev),),
             device_id_type=MESH,
         )
 
-    def pack(r, source):
-        for q in ORDER:
-            for g in range(GMAX):
-                sends[r, q, pl.ds(g, 1), :] = source[pl.ds(lists_s[0, q, g], 1), :]
-            if r > 0:
-                packet(r, q).start()
-
     def await_ghosts(r):
         for q in ORDER:
-            packet(r, q).wait_recv()
+            packet(r, q, sends.at[0, 0]).wait_recv()
 
     def lane_sums(total):
         return jnp.sum(total.T, axis=0, keepdims=True)
@@ -192,68 +181,111 @@
 
         def group(i, carry):
             for s in range(GROUP):
-                b = i * GROUP + s
-                mine = source[pl.ds(b, 1), :]
-                here = lane_sums(blocks[b, 0] * mine)
+                p = i * GROUP + s
+                mine = source[pl.ds(p, 1), :]
+                here = lane_sums(blocks[row_s[p], 0] * mine)
                 if r == 0:
-                    kept = rate[pl.ds(b, 1), :] * mine * (1.0 - mine)
+                    kept = rate[pl.ds(p, 1), :] * mine * (1.0 - mine)
                 else:
-                    kept = slope8[pl.ds(b, 1), :] * mine
-                fixed[pl.ds(b, 1), :] = kept - here
+                    kept = slope8[pl.ds(p, 1), :] * mine
+                fixed[pl.ds(p, 1), :] = kept - here
             return carry
 
         lax.fori_loop(0, BDEV // GROUP, group, 0)
 
-    def product(r):
+    def product(r, low, high):
         x = xs[r]
-        for b in range(BDEV):
+        for p in range(low, high):
             total = None
+            b = row_s[p]
             for t in range(1, NNZB):
-                row = x[pl.ds(index_s[b * NNZB + t], 8, stride=0), :]
+                row = x[pl.ds(index_s[p * NNZB + t], 8, stride=0), :]
                 term = blocks[b, t].reshape(16, 8, BLK) * row[None]
                 total = term if total is None else total + term
-            whole = fixed[pl.ds(b, 1), :] - lane_sums(total.reshape(BLK, BLK))
-            ys[r, pl.ds(b, 1), :] = whole if r == 0 else whole * SCALE
+            whole = fixed[pl.ds(p, 1), :] - lane_sums(total.reshape(BLK, BLK))
+            whole = whole if r == 0 else whole * SCALE
+            ys[r, pl.ds(p, 1), :] = whole
+            if r + 1 < ROUNDS:
+                xs[r + 1][pl.ds(p, 1), :] = whole
+
+    def turn(r):
+        product(r, 0, GMAX)
+        n = r + 1
+        if n < ROUNDS:
+            packet(n, urgent, ys.at[r, pl.ds(0, GMAX), :]).start()
+        product(r, GMAX, BDEV)
+        if n < ROUNDS:
+            for k in range(1, 4):
+                q = lax.rem(urgent + k, 4)
+                for g in range(GMAX):
+                    sends[n, k, pl.ds(g, 1), :] = ys[r, pl.ds(pick_s[q * GMAX + g], 1), :]
+                packet(n, q, sends.at[n, k]).start()
 
     small[0].wait()
     small[1].wait()
-    pack(0, conc)
+    for q in ORDER:
+        for g in range(GMAX):
+            sends[0, q, pl.ds(g, 1), :] = conc_in[pl.ds(lists_s[0, q, g], 1), :]
     pl.semaphore_wait(barrier, len(greeted))
     for q in ORDER:
-        packet(0, q).start()
+        packet(0, q, sends.at[0, q]).start()
     for o in z_line:
         pl.semaphore_signal(known_z, inc=1, device_id=(at(o),), device_id_type=MESH)
-    xs[0][pl.ds(0, BDEV), :] = conc[...]
     for x in xs:
         x[pl.ds(ZERO_ROW, 8), :] = jnp.zeros((8, BLK), jnp.float32)
     for copy in small[2:]:
         copy.wait()
-    slope8[...] = rate[...] * (1.0 - 2.0 * conc[...]) + SHIFT
-
-    def remap(b, carry):
+
+    def find(b, others):
+        found = 0
+        for g in range(GMAX):
+            found = jnp.where(lists_s[0, urgent, g] == b, g + 1, found)
+        place_s[b] = jnp.where(found > 0, found - 1, jnp.minimum(GMAX + others, BDEV - 1))
+        return others + jnp.where(found > 0, 0, 1)
+
+    lax.fori_loop(0, BDEV, find, 0)
+
+    def order(p, carry):
+        b = 0
+        for i in range(BDEV):
+            b = jnp.where(place_s[i] == p, i, b)
+        row_s[p] = b
+        conc[pl.ds(p, 1), :] = conc_in[pl.ds(b, 1), :]
+        rate[pl.ds(p, 1), :] = rate_in[pl.ds(b, 1), :]
+        xs[0][pl.ds(p, 1), :] = conc_in[pl.ds(b, 1), :]
         length = lens_s[b]
         for t in range(1, NNZB):
-            index_s[b * NNZB + t] = jnp.where(t < length, cols_s[t, b], ZERO_ROW)
+            col = cols_s[t, b]
+            moved = jnp.where(col < BDEV, place_s[jnp.clip(col, 0, BDEV - 1)], jnp.minimum(col, ZERO_ROW))
+            index_s[p * NNZB + t] = jnp.where(t < length, moved, ZERO_ROW)
         return carry
 
-    lax.fori_loop(0, BDEV, remap, 0)
+    lax.fori_loop(0, BDEV, order, 0)
+
+    def choose(g, carry):
+        for q in range(4):
+            pick_s[q * GMAX + g] = place_s[lists_s[0, q, g]]
+        return carry
+
+    lax.fori_loop(0, GMAX, choose, 0)
+    slope8[...] = rate[...] * (1.0 - 2.0 * conc[...]) + SHIFT
     for chunk in chunks:
         chunk.wait()
     own_part(0)
     await_ghosts(0)
-    product(0)
+    turn(0)
 
     def broadcast_gram(slot, products):
         rows = [jnp.sum(p, axis=0, keepdims=True) for p in products]
         rows = rows + [jnp.zeros((BLK - len(rows), BLK), jnp.float32)]
         gram_row[slot] = jnp.sum(jnp.concatenate(rows, axis=0).T, axis=0, keepdims=True)
-        for o in far_first():
+        for k in range(ndev - 1):
             pltpu.make_async_remote_copy(
                 src_ref=gram_row.at[slot],
                 dst_ref=arrivals.at[slot, me],
                 send_sem=ar_send.at[slot],
                 recv_sem=ar_recv.at[slot],
-                device_id=(at(o),),
+                device_id=(jnp.where(me <= k, k + 1, k),),
                 device_id_type=MESH,
             ).start()
 
@@ -269,8 +301,6 @@
     substep = jnp.full((1, BLK), step_s[0] * 0.5, jnp.float32)
     us = None
     for r in range(1, ROUNDS):
-        pack(r, ys.at[r - 1])
-        xs[r][pl.ds(0, BDEV), :] = ys[r - 1]
         if r == 1:
             pl.semaphore_wait(known_z, 3)
             for o in y_line:
@@ -300,14 +330,16 @@
                 conc[...] + first_weights[0] * w[0] + first_weights[1] * w[1] + first_weights[2] * w[2]
             )
         await_ghosts(r)
-        product(r)
+        turn(r)
     last = tail + d[3] * ys[ROUNDS - 1]
     broadcast_gram(1, partial + [us[i] * last for i in range(3)])
     second = arnoldi_weights(collect_gram(1), substep)
-    result[...] = base + second[0] * us[0] + second[1] * us[1] + second[2] * us[2]
+    ordered[...] = base + second[0] * us[0] + second[1] * us[1] + second[2] * us[2]
+    for b in range(BDEV):
+        result[pl.ds(b, 1), :] = ordered[pl.ds(place_s[b], 1), :]
     for r in range(ROUNDS):
         for q in range(4):
-            packet(r, q).wait_send()
+            packet(r, q, sends.at[0, 0]).wait_send()
     for slot in range(2):
         whole = arrivals.at[slot, pl.ds(0, ndev - 1)]
         pltpu.make_async_copy(whole, whole, ar_send.at[slot]).wait()
@@ -328,16 +360,22 @@
                 pltpu.VMEM((BDEV, BLK), f32),
                 pltpu.VMEM((BDEV, BLK), f32),
                 pltpu.VMEM((BDEV, BLK), f32),
+                pltpu.VMEM((BDEV, BLK), f32),
+                pltpu.VMEM((BDEV, BLK), f32),
                 pltpu.VMEM((BDEV, NNZB, BLK, BLK), f32),
                 pltpu.VMEM((ROUNDS, BDEV, BLK), f32),
                 pltpu.VMEM((ROUNDS, 4, GMAX, BLK), f32),
                 pltpu.VMEM((2, 1, BLK), f32),
                 pltpu.VMEM((2, ndev, 1, BLK), f32),
+                pltpu.VMEM((BDEV, BLK), f32),
                 pltpu.SMEM((1,), f32),
                 pltpu.SMEM((NNZB, BDEV), i32),
                 pltpu.SMEM((BDEV,), i32),
                 pltpu.SMEM((1, 4, GMAX), i32),
                 pltpu.SMEM((BDEV * NNZB,), i32),
+                pltpu.SMEM((BDEV,), i32),
+                pltpu.SMEM((BDEV,), i32),
+                pltpu.SMEM((4 * GMAX,), i32),
             ]
             + [pltpu.VMEM((XROWS, BLK), f32)] * ROUNDS
             + [

time: 60.2 us -> 58 us (0.963)
  Pallas kernels: 58.8 us -> 56.6 us
    pallas_call x1, Pallas kernels: 58.8 us -> 56.6 us  [step(): pl.pallas_call(lambda *refs: kernel(ndev, *refs), out_shape=pltpu.VMEM((B...]
where the time goes in v3:
time: 58 us; the launch traced here: 57.9 us
  Pallas kernels  56.6 us (98%)
  between operations  0.66 us (1%)
  local copies, waits for them, and re-layouts  0.61 us (1%)
    pallas_call x1, Pallas kernels, step(): pl.pallas_call(lambda *refs: kernel(ndev, *refs), out_shape=pltpu.VMEM((B...  56.6 us

profile of v3, /device:TPU:1, one launch (start us, length us, event | category | flops | bytes accessed | tf_op | source)
XLA Modules:
  0.0 57.9 jit_solution(8807160491990930567)
XLA Ops:
  0.7 56.6 %rosenbrock.1 = f32[32,128]{1,0:T(8,128)S(1)} custom-call(f32[32,128]{1,0:T(8,128)} %refs_0_.1, f32[32,128]{1,0:T(8,128)} %refs_1_.1, f32[1]{0:T(128)S(6)} %copy.10.refs_2_, f32[32,5,128,128]{3,2,1,0:T(8,128)} %refs_3_.1, s32[5,32]{1,0:T(8,128)} %bitcast.1, s32[32]{0:T(128)} %refs_5_.1, s32[1,4,16]{2,1,0:T(4,128)} %refs_6_.1), custom_call_target="tpu_custom_call" | custom-call | tf_op jit(solution)/shard_map/rosenbrock/pallas_call | solution.py:353
  57.3 0.6 %copy.9 = f32[32,128]{1,0:T(8,128)} copy(f32[32,128]{1,0:T(8,128)S(1)} %rosenbrock.1) | data formatting | bytes 32768

commit v4 on v3

--- a/solution.py
+++ b/solution.py
@@ -19,6 +19,10 @@
 CHUNK = 4
 ZERO_ROW = BDEV + 4 * GMAX
 XROWS = ZERO_ROW + 8
+RELAY_ROW = XROWS
+RELAY_A = 7
+RELAY_B = 103
+RELAYED = ((2, 0), (1, 1), (1, 0))
 PAIRS = ((0, 0), (0, 1), (0, 2), (1, 1), (1, 2), (2, 2), (0, 3), (1, 3), (2, 3))
 MESH = pl.DeviceIdType.MESH
 
@@ -116,7 +120,7 @@
     (conc_in, rate_in, conc, rate, slope8, fixed, blocks, ys, sends, gram_row, arrivals, ordered) = scratch[:12]
     (step_s, cols_s, lens_s, lists_s, index_s, place_s, row_s, pick_s) = scratch[12:20]
     xs = scratch[20 : 20 + ROUNDS]
-    in_sems, block_sems, send_sems, recv_sems, ar_send, ar_recv, known_z, known_y = scratch[20 + ROUNDS :]
+    in_sems, block_sems, send_sems, recv_sems, ar_send, ar_recv, relay_sems, known_z, known_y = scratch[20 + ROUNDS :]
     me = lax.axis_index("dom")
 
     def near(o):
@@ -136,11 +140,6 @@
     row_line = [(0, 0, x, c) for x in range(4) for c in range(2) if (x, c) != (0, 0)]
     z_line = [(0, d, 0, 0) for d in (1, 2, 3)]
     y_line = [(d, 0, 0, 0) for d in (1, 2, 3)]
-
-    barrier = pltpu.get_barrier_semaphore()
-    greeted = [near(OFFSETS[q]) for q in ORDER] + [at(o) for o in z_line + y_line + row_line]
-    for device in greeted:
-        pl.semaphore_signal(barrier, inc=1, device_id=(device,), device_id_type=MESH)
 
     small = [
         pltpu.make_async_copy(lists_hbm, lists_s, in_sems.at[0]),
@@ -150,7 +149,18 @@
         pltpu.make_async_copy(rate_hbm, rate_in, in_sems.at[4]),
         pltpu.make_async_copy(step_hbm, step_s, in_sems.at[5]),
     ]
-    for copy in small:
+    small[0].start()
+    small[1].start()
+
+    barrier = pltpu.get_barrier_semaphore()
+    greeted = [
+        jnp.where(me + OFFSETS[q] >= ndev, RELAY_B, near(OFFSETS[q])) for q in ORDER
+    ] + [at(o) for o in z_line + y_line + row_line]
+    for device in greeted:
+        pl.semaphore_signal(barrier, inc=1, device_id=(device,), device_id_type=MESH)
+    greetings = len(greeted) + jnp.where(me == RELAY_B, 3, 0) - jnp.maximum(2 - me, 0)
+
+    for copy in small[2:]:
         copy.start()
     chunks = []
     for c in range(BDEV // CHUNK):
@@ -226,9 +236,50 @@
     for q in ORDER:
         for g in range(GMAX):
             sends[0, q, pl.ds(g, 1), :] = conc_in[pl.ds(lists_s[0, q, g], 1), :]
-    pl.semaphore_wait(barrier, len(greeted))
+    pl.semaphore_wait(barrier, greetings)
     for q in ORDER:
-        packet(0, q, sends.at[0, q]).start()
+        relayed = me + OFFSETS[q] < 0
+        slot = q + 2 * me
+        pltpu.make_async_remote_copy(
+            src_ref=sends.at[0, q],
+            dst_ref=xs[0].at[
+                pl.ds(
+                    pl.multiple_of(
+                        jnp.where(relayed, RELAY_ROW + slot * GMAX, BDEV + q * GMAX), 8
+                    ),
+                    GMAX,
+                ),
+                :,
+            ],
+            send_sem=send_sems.at[0, q],
+            recv_sem=recv_sems.at[jnp.where(relayed, ROUNDS, 0), jnp.where(relayed, slot, q)],
+            device_id=(jnp.where(relayed, RELAY_A, near(OFFSETS[q])),),
+            device_id_type=MESH,
+        ).start()
+
+    def forward(i):
+        before_end, q = RELAYED[i]
+        first = me == RELAY_A
+        here = xs[0].at[pl.ds(RELAY_ROW + i * GMAX, GMAX), :]
+        row = jnp.where(first, RELAY_ROW + i * GMAX, BDEV + q * GMAX)
+        return pltpu.make_async_remote_copy(
+            src_ref=here,
+            dst_ref=xs[0].at[pl.ds(pl.multiple_of(row, 8), GMAX), :],
+            send_sem=relay_sems.at[i],
+            recv_sem=recv_sems.at[jnp.where(first, ROUNDS, 0), jnp.where(first, i, q)],
+            device_id=(jnp.where(first, RELAY_B, ndev - before_end),),
+            device_id_type=MESH,
+        )
+
+    is_relay = (me == RELAY_A) | (me == RELAY_B)
+
+    @pl.when(is_relay)
+    def _():
+        for i in range(len(RELAYED)):
+            here = xs[0].at[pl.ds(RELAY_ROW + i * GMAX, GMAX), :]
+            pltpu.make_async_copy(here, here, recv_sems.at[ROUNDS, i]).wait()
+            forward(i).start()
+
     for o in z_line:
         pl.semaphore_signal(known_z, inc=1, device_id=(at(o),), device_id_type=MESH)
     for x in xs:
@@ -340,6 +391,12 @@
     for r in range(ROUNDS):
         for q in range(4):
             packet(r, q, sends.at[0, 0]).wait_send()
+
+    @pl.when(is_relay)
+    def _():
+        for i in range(len(RELAYED)):
+            forward(i).wait_send()
+
     for slot in range(2):
         whole = arrivals.at[slot, pl.ds(0, ndev - 1)]
         pltpu.make_async_copy(whole, whole, ar_send.at[slot]).wait()
@@ -377,14 +434,16 @@
                 pltpu.SMEM((BDEV,), i32),
                 pltpu.SMEM((4 * GMAX,), i32),
             ]
-            + [pltpu.VMEM((XROWS, BLK), f32)] * ROUNDS
+            + [pltpu.VMEM((XROWS + len(RELAYED) * GMAX, BLK), f32)]
+            + [pltpu.VMEM((XROWS, BLK), f32)] * (ROUNDS - 1)
             + [
                 pltpu.SemaphoreType.DMA((6,)),
                 pltpu.SemaphoreType.DMA((BDEV // CHUNK,)),
                 pltpu.SemaphoreType.DMA((ROUNDS, 4)),
-                pltpu.SemaphoreType.DMA((ROUNDS, 4)),
+                pltpu.SemaphoreType.DMA((ROUNDS + 1, 4)),
                 pltpu.SemaphoreType.DMA((2,)),
                 pltpu.SemaphoreType.DMA((2,)),
+                pltpu.SemaphoreType.DMA((len(RELAYED),)),
                 pltpu.SemaphoreType.REGULAR,
                 pltpu.SemaphoreType.REGULAR,
             ],

time: 58 us -> 56.1 us (0.967)
  Pallas kernels: 56.6 us -> 54.7 us
    pallas_call x1, Pallas kernels: 56.6 us -> 54.7 us  [step(): pl.pallas_call(lambda *refs: kernel(ndev, *refs), out_shape=pltpu.VMEM((B...]
where the time goes in v4:
time: 56.1 us; the launch traced here: 56 us
  Pallas kernels  54.7 us (98%)
  between operations  0.66 us (1%)
  local copies, waits for them, and re-layouts  0.61 us (1%)
    pallas_call x1, Pallas kernels, step(): pl.pallas_call(lambda *refs: kernel(ndev, *refs), out_shape=pltpu.VMEM((B...  54.7 us

profile of v4, /device:TPU:1, one launch (start us, length us, event | category | flops | bytes accessed | tf_op | source)
XLA Modules:
  0.0 56.0 jit_solution(3224746813990810129)
XLA Ops:
  0.7 54.7 %rosenbrock.1 = f32[32,128]{1,0:T(8,128)S(1)} custom-call(f32[32,128]{1,0:T(8,128)} %refs_0_.1, f32[32,128]{1,0:T(8,128)} %refs_1_.1, f32[1]{0:T(128)S(6)} %copy.10.refs_2_, f32[32,5,128,128]{3,2,1,0:T(8,128)} %refs_3_.1, s32[5,32]{1,0:T(8,128)} %bitcast.1, s32[32]{0:T(128)} %refs_5_.1, s32[1,4,16]{2,1,0:T(4,128)} %refs_6_.1), custom_call_target="tpu_custom_call" | custom-call | tf_op jit(solution)/shard_map/rosenbrock/pallas_call | solution.py:410
  55.4 0.6 %copy.9 = f32[32,128]{1,0:T(8,128)} copy(f32[32,128]{1,0:T(8,128)S(1)} %rosenbrock.1) | data formatting | bytes 32768

commit v5 on v4

--- a/solution.py
+++ b/solution.py
@@ -120,26 +120,14 @@
     (conc_in, rate_in, conc, rate, slope8, fixed, blocks, ys, sends, gram_row, arrivals, ordered) = scratch[:12]
     (step_s, cols_s, lens_s, lists_s, index_s, place_s, row_s, pick_s) = scratch[12:20]
     xs = scratch[20 : 20 + ROUNDS]
-    in_sems, block_sems, send_sems, recv_sems, ar_send, ar_recv, relay_sems, known_z, known_y = scratch[20 + ROUNDS :]
+    in_sems, block_sem, send_sem, recv_sems, ar_send, ar_recv, relay_sem, known = scratch[20 + ROUNDS :]
     me = lax.axis_index("dom")
 
     def near(o):
         return lax.rem(me + (o + ndev), ndev)
 
     my_core, my_x = lax.rem(me, 2), lax.rem(me // 2, 4)
-    my_z, my_y = lax.rem(me // 8, 4), me // 32
-    at_y = [lax.rem(my_y + d, 4) * 32 for d in range(4)]
-    at_z = [lax.rem(my_z + d, 4) * 8 for d in range(4)]
-    at_x = [lax.rem(my_x + d, 4) * 2 for d in range(4)]
-    at_core = [my_core, 1 - my_core]
     urgent = jnp.where(my_x < 2, 0, 3 - my_core)
-
-    def at(o):
-        return at_y[o[0]] + at_z[o[1]] + at_x[o[2]] + at_core[o[3]]
-
-    row_line = [(0, 0, x, c) for x in range(4) for c in range(2) if (x, c) != (0, 0)]
-    z_line = [(0, d, 0, 0) for d in (1, 2, 3)]
-    y_line = [(d, 0, 0, 0) for d in (1, 2, 3)]
 
     small = [
         pltpu.make_async_copy(lists_hbm, lists_s, in_sems.at[0]),
@@ -149,39 +137,51 @@
         pltpu.make_async_copy(rate_hbm, rate_in, in_sems.at[4]),
         pltpu.make_async_copy(step_hbm, step_s, in_sems.at[5]),
     ]
-    small[0].start()
-    small[1].start()
+    for copy in small:
+        copy.start()
 
     barrier = pltpu.get_barrier_semaphore()
-    greeted = [
-        jnp.where(me + OFFSETS[q] >= ndev, RELAY_B, near(OFFSETS[q])) for q in ORDER
-    ] + [at(o) for o in z_line + y_line + row_line]
-    for device in greeted:
+
+    def greet(device):
         pl.semaphore_signal(barrier, inc=1, device_id=(device,), device_id_type=MESH)
-    greetings = len(greeted) + jnp.where(me == RELAY_B, 3, 0) - jnp.maximum(2 - me, 0)
-
-    for copy in small[2:]:
-        copy.start()
-    chunks = []
+
+    for q in ORDER:
+        greet(jnp.where(me + OFFSETS[q] >= ndev, RELAY_B, near(OFFSETS[q])))
+
+    @pl.when(me == RELAY_A)
+    def _():
+        greet(0)
+        greet(1)
+
+    @pl.when(me == RELAY_B)
+    def _():
+        greet(RELAY_A)
+
+    greetings = (
+        4
+        + jnp.where(me == RELAY_B, 3, 0)
+        + jnp.where(me == RELAY_A, 1, 0)
+        - jnp.where(me == 0, 1, 0)
+    )
+
     for c in range(BDEV // CHUNK):
         part = pl.ds(c * CHUNK, CHUNK)
-        chunks.append(pltpu.make_async_copy(blocks_hbm.at[part], blocks.at[part], block_sems.at[c]))
-        chunks[-1].start()
+        pltpu.make_async_copy(blocks_hbm.at[part], blocks.at[part], block_sem).start()
 
     def packet(r, q, source):
         offset = jnp.where(q < 2, q - 2, q - 1)
         return pltpu.make_async_remote_copy(
             src_ref=source,
             dst_ref=xs[r].at[pl.ds(pl.multiple_of(BDEV + q * GMAX, 8), GMAX), :],
-            send_sem=send_sems.at[r, q],
-            recv_sem=recv_sems.at[r, q],
+            send_sem=send_sem,
+            recv_sem=recv_sems.at[r],
             device_id=(lax.rem(me + offset + ndev, ndev),),
             device_id_type=MESH,
         )
 
     def await_ghosts(r):
-        for q in ORDER:
-            packet(r, q, sends.at[0, 0]).wait_recv()
+        part = xs[r].at[pl.ds(BDEV, 4 * GMAX), :]
+        pltpu.make_async_copy(part, part, recv_sems.at[r]).wait()
 
     def lane_sums(total):
         return jnp.sum(total.T, axis=0, keepdims=True)
@@ -251,8 +251,8 @@
                 ),
                 :,
             ],
-            send_sem=send_sems.at[0, q],
-            recv_sem=recv_sems.at[jnp.where(relayed, ROUNDS, 0), jnp.where(relayed, slot, q)],
+            send_sem=send_sem,
+            recv_sem=recv_sems.at[jnp.where(relayed, ROUNDS, 0)],
             device_id=(jnp.where(relayed, RELAY_A, near(OFFSETS[q])),),
             device_id_type=MESH,
         ).start()
@@ -265,23 +265,21 @@
         return pltpu.make_async_remote_copy(
             src_ref=here,
             dst_ref=xs[0].at[pl.ds(pl.multiple_of(row, 8), GMAX), :],
-            send_sem=relay_sems.at[i],
-            recv_sem=recv_sems.at[jnp.where(first, ROUNDS, 0), jnp.where(first, i, q)],
+            send_sem=relay_sem,
+            recv_sem=recv_sems.at[jnp.where(first, ROUNDS, 0)],
             device_id=(jnp.where(first, RELAY_B, ndev - before_end),),
             device_id_type=MESH,
         )
 
+    relay_part = xs[0].at[pl.ds(RELAY_ROW, len(RELAYED) * GMAX), :]
     is_relay = (me == RELAY_A) | (me == RELAY_B)
 
     @pl.when(is_relay)
     def _():
+        pltpu.make_async_copy(relay_part, relay_part, recv_sems.at[ROUNDS]).wait()
         for i in range(len(RELAYED)):
-            here = xs[0].at[pl.ds(RELAY_ROW + i * GMAX, GMAX), :]
-            pltpu.make_async_copy(here, here, recv_sems.at[ROUNDS, i]).wait()
             forward(i).start()
 
-    for o in z_line:
-        pl.semaphore_signal(known_z, inc=1, device_id=(at(o),), device_id_type=MESH)
     for x in xs:
         x[pl.ds(ZERO_ROW, 8), :] = jnp.zeros((8, BLK), jnp.float32)
     for copy in small[2:]:
@@ -295,23 +293,27 @@
         return others + jnp.where(found > 0, 0, 1)
 
     lax.fori_loop(0, BDEV, find, 0)
-
-    def order(p, carry):
-        b = 0
-        for i in range(BDEV):
-            b = jnp.where(place_s[i] == p, i, b)
+    for c in range(BDEV, ZERO_ROW):
+        place_s[c] = c
+
+    def settle(p, b):
         row_s[p] = b
         conc[pl.ds(p, 1), :] = conc_in[pl.ds(b, 1), :]
         rate[pl.ds(p, 1), :] = rate_in[pl.ds(b, 1), :]
         xs[0][pl.ds(p, 1), :] = conc_in[pl.ds(b, 1), :]
         length = lens_s[b]
         for t in range(1, NNZB):
-            col = cols_s[t, b]
-            moved = jnp.where(col < BDEV, place_s[jnp.clip(col, 0, BDEV - 1)], jnp.minimum(col, ZERO_ROW))
-            index_s[p * NNZB + t] = jnp.where(t < length, moved, ZERO_ROW)
+            index_s[p * NNZB + t] = jnp.where(t < length, place_s[cols_s[t, b]], ZERO_ROW)
+
+    def settle_pair(g, carry):
+        settle(g, lists_s[0, urgent, g])
+        b = g
+        for i in range(1, GMAX + 1):
+            b = jnp.where(place_s[g + i] == GMAX + g, g + i, b)
+        settle(GMAX + g, b)
         return carry
 
-    lax.fori_loop(0, BDEV, order, 0)
+    lax.fori_loop(0, GMAX, settle_pair, 0)
 
     def choose(g, carry):
         for q in range(4):
@@ -320,21 +322,26 @@
 
     lax.fori_loop(0, GMAX, choose, 0)
     slope8[...] = rate[...] * (1.0 - 2.0 * conc[...]) + SHIFT
-    for chunk in chunks:
-        chunk.wait()
+    pltpu.make_async_copy(blocks, blocks, block_sem).wait()
     own_part(0)
     await_ghosts(0)
     turn(0)
 
-    def broadcast_gram(slot, products):
-        rows = [jnp.sum(p, axis=0, keepdims=True) for p in products]
-        rows = rows + [jnp.zeros((BLK - len(rows), BLK), jnp.float32)]
-        gram_row[slot] = jnp.sum(jnp.concatenate(rows, axis=0).T, axis=0, keepdims=True)
+    lane = lax.broadcasted_iota(jnp.int32, (1, BLK), 1)
+
+    def sums_row(products, first, row):
+        for e, p in enumerate(products, first):
+            total = jnp.sum(jnp.sum(p, axis=0, keepdims=True), axis=1, keepdims=True)
+            row = jnp.where(lane == e, total, row)
+        return row
+
+    def broadcast_gram(slot, row):
+        gram_row[slot] = row
         for k in range(ndev - 1):
             pltpu.make_async_remote_copy(
                 src_ref=gram_row.at[slot],
                 dst_ref=arrivals.at[slot, me],
-                send_sem=ar_send.at[slot],
+                send_sem=ar_send,
                 recv_sem=ar_recv.at[slot],
                 device_id=(jnp.where(me <= k, k + 1, k),),
                 device_id_type=MESH,
@@ -342,25 +349,34 @@
 
     def collect_gram(slot):
         whole = arrivals.at[slot, pl.ds(0, ndev - 1)]
-        pltpu.make_async_copy(whole, whole, ar_recv.at[slot]).wait()
+        with jax.named_scope(f"collect{slot}"):
+            pltpu.make_async_copy(whole, whole, ar_recv.at[slot]).wait()
         arrivals[slot, me] = gram_row[slot]
-        total = jnp.sum(arrivals[slot], axis=0)
+        parts = [arrivals[slot, i] for i in range(ndev)]
+        while len(parts) > 1:
+            parts = [a + b for a, b in zip(parts[::2], parts[1::2])]
+        total = parts[0]
         return {
             pair: jnp.broadcast_to(total[:, e : e + 1], (1, BLK)) for e, pair in enumerate(PAIRS)
         }
 
+    def meet(step):
+        for o in (2 << step, -(2 << step)):
+            pl.semaphore_signal(known.at[step], inc=1, device_id=(near(o),), device_id_type=MESH)
+
+    zero_row = jnp.zeros((1, BLK), jnp.float32)
+    meet(0)
     substep = jnp.full((1, BLK), step_s[0] * 0.5, jnp.float32)
     us = None
     for r in range(1, ROUNDS):
-        if r == 1:
-            pl.semaphore_wait(known_z, 3)
-            for o in y_line:
-                pl.semaphore_signal(known_y, inc=1, device_id=(at(o),), device_id_type=MESH)
+        if r <= 4:
+            pl.semaphore_wait(known.at[r - 1], 2)
+            meet(r)
         own_part(r)
         if r == 4:
-            pl.semaphore_wait(known_y, 3)
+            pl.semaphore_wait(known.at[4], 2)
             w = [ys[k] for k in range(4)]
-            broadcast_gram(0, [w[i] * w[j] for i, j in PAIRS])
+            broadcast_gram(0, sums_row([w[i] * w[j] for i, j in PAIRS], 0, zero_row))
         if r == ROUNDS - 1:
             w = [ys[k] for k in range(6)]
             first_weights = arnoldi_weights(collect_gram(0), substep)
@@ -376,30 +392,26 @@
             d[0] = d[0] + 1.0
             us = [d[0] * w[k] + d[1] * w[k + 1] + d[2] * w[k + 2] + d[3] * w[k + 3] for k in range(3)]
             tail = d[0] * w[3] + d[1] * w[4] + d[2] * w[5]
-            partial = [us[i] * us[j] for i, j in PAIRS[:6]]
+            partial = sums_row([us[i] * us[j] for i, j in PAIRS[:6]], 0, zero_row)
             base = (
                 conc[...] + first_weights[0] * w[0] + first_weights[1] * w[1] + first_weights[2] * w[2]
             )
         await_ghosts(r)
         turn(r)
     last = tail + d[3] * ys[ROUNDS - 1]
-    broadcast_gram(1, partial + [us[i] * last for i in range(3)])
+    broadcast_gram(1, sums_row([us[i] * last for i in range(3)], 6, partial))
     second = arnoldi_weights(collect_gram(1), substep)
     ordered[...] = base + second[0] * us[0] + second[1] * us[1] + second[2] * us[2]
     for b in range(BDEV):
         result[pl.ds(b, 1), :] = ordered[pl.ds(place_s[b], 1), :]
-    for r in range(ROUNDS):
-        for q in range(4):
-            packet(r, q, sends.at[0, 0]).wait_send()
+    pltpu.make_async_copy(sends, sends, send_sem).wait()
 
     @pl.when(is_relay)
     def _():
-        for i in range(len(RELAYED)):
-            forward(i).wait_send()
-
-    for slot in range(2):
-        whole = arrivals.at[slot, pl.ds(0, ndev - 1)]
-        pltpu.make_async_copy(whole, whole, ar_send.at[slot]).wait()
+        pltpu.make_async_copy(relay_part, relay_part, relay_sem).wait()
+
+    whole = arrivals.at[:, pl.ds(0, ndev - 1)]
+    pltpu.make_async_copy(whole, whole, ar_send).wait()
 
 
 def solution(mesh):
@@ -430,7 +442,7 @@
                 pltpu.SMEM((BDEV,), i32),
                 pltpu.SMEM((1, 4, GMAX), i32),
                 pltpu.SMEM((BDEV * NNZB,), i32),
-                pltpu.SMEM((BDEV,), i32),
+                pltpu.SMEM((ZERO_ROW,), i32),
                 pltpu.SMEM((BDEV,), i32),
                 pltpu.SMEM((4 * GMAX,), i32),
             ]
@@ -438,14 +450,13 @@
             + [pltpu.VMEM((XROWS, BLK), f32)] * (ROUNDS - 1)
             + [
                 pltpu.SemaphoreType.DMA((6,)),
-                pltpu.SemaphoreType.DMA((BDEV // CHUNK,)),
-                pltpu.SemaphoreType.DMA((ROUNDS, 4)),
-                pltpu.SemaphoreType.DMA((ROUNDS + 1, 4)),
+                pltpu.SemaphoreType.DMA,
+                pltpu.SemaphoreType.DMA,
+                pltpu.SemaphoreType.DMA((ROUNDS + 1,)),
+                pltpu.SemaphoreType.DMA,
                 pltpu.SemaphoreType.DMA((2,)),
-                pltpu.SemaphoreType.DMA((2,)),
-                pltpu.SemaphoreType.DMA((len(RELAYED),)),
-                pltpu.SemaphoreType.REGULAR,
-                pltpu.SemaphoreType.REGULAR,
+                pltpu.SemaphoreType.DMA,
+                pltpu.SemaphoreType.REGULAR((5,)),
             ],
             compiler_params=pltpu.CompilerParams(collective_id=0, has_side_effects=True),
             name="rosenbrock",

time: 56.1 us -> 54 us (0.963)
  Pallas kernels: 54.7 us -> 52.6 us
    pallas_call x1, Pallas kernels: 54.7 us -> 52.6 us  [step(): pl.pallas_call(lambda *refs: kernel(ndev, *refs), out_shape=pltpu.VMEM((B...]
where the time goes in v5:
time: 54 us; the launch traced here: 53.9 us
  Pallas kernels  52.6 us (97%)
  between operations  0.66 us (1%)
  local copies, waits for them, and re-layouts  0.61 us (1%)
    pallas_call x1, Pallas kernels, step(): pl.pallas_call(lambda *refs: kernel(ndev, *refs), out_shape=pltpu.VMEM((B...  52.6 us

profile of v5, /device:TPU:1, one launch (start us, length us, event | category | flops | bytes accessed | tf_op | source)
XLA Modules:
  0.0 53.9 jit_solution(12802831410903966187)
XLA Ops:
  0.7 52.6 %rosenbrock.1 = f32[32,128]{1,0:T(8,128)S(1)} custom-call(f32[32,128]{1,0:T(8,128)} %refs_0_.1, f32[32,128]{1,0:T(8,128)} %refs_1_.1, f32[1]{0:T(128)S(6)} %copy.10.refs_2_, f32[32,5,128,128]{3,2,1,0:T(8,128)} %refs_3_.1, s32[5,32]{1,0:T(8,128)} %bitcast.1, s32[32]{0:T(128)} %refs_5_.1, s32[1,4,16]{2,1,0:T(4,128)} %refs_6_.1), custom_call_target="tpu_custom_call" | custom-call | tf_op jit(solution)/shard_map/rosenbrock/pallas_call | solution.py:422
  53.3 0.6 %copy.9 = f32[32,128]{1,0:T(8,128)} copy(f32[32,128]{1,0:T(8,128)S(1)} %rosenbrock.1) | data formatting | bytes 32768

commit v6 on v5

--- a/solution.py
+++ b/solution.py
@@ -80,32 +80,31 @@
             vectors.append([r * inverse for r in rest])
     small = substep * (1.0 / 64.0)
     A = [[None if H[i][j] is None else H[i][j] * small for j in range(3)] for i in range(3)]
-    one = jnp.ones_like(substep)
-    Pm = [[one if i == j else zero for j in range(3)] for i in range(3)]
-    q = [zero] * 3
+    sublane = lax.broadcasted_iota(jnp.int32, substep.shape, 0)
+    unit = [jnp.where(sublane == i, 1.0, 0.0) for i in range(4)]
+    rows = unit[:3]
     for degree in range(12, 0, -1):
-        inv = 1.0 / degree
-        newP = [[None] * 3 for _ in range(3)]
-        newq = [None] * 3
+        new = []
         for i in range(3):
-            ks = [k for k in range(3) if A[i][k] is not None]
-            for j in range(3):
-                total = A[i][ks[0]] * Pm[ks[0]][j]
-                for k in ks[1:]:
-                    total = total + A[i][k] * Pm[k][j]
-                total = total * inv
-                newP[i][j] = total + 1.0 if i == j else total
-            total = A[i][ks[0]] * q[ks[0]]
-            for k in ks[1:]:
-                total = total + A[i][k] * q[k]
-            if i == 0:
-                total = total + (1.0 / 64.0)
-            newq[i] = total * inv
-        Pm, q = newP, newq
+            total = unit[3] * (1.0 / 64.0) if i == 0 else None
+            for k in range(3):
+                if A[i][k] is not None:
+                    term = A[i][k] * rows[k]
+                    total = term if total is None else total + term
+            new.append(unit[i] + total * (1.0 / degree))
+        rows = new
+
+    def column(row, k):
+        return jnp.broadcast_to(row[k : k + 1, :], substep.shape)
+
     for _ in range(6):
-        newP = [[Pm[i][0] * Pm[0][j] + Pm[i][1] * Pm[1][j] + Pm[i][2] * Pm[2][j] for j in range(3)] for i in range(3)]
-        q = [Pm[i][0] * q[0] + Pm[i][1] * q[1] + Pm[i][2] * q[2] + q[i] for i in range(3)]
-        Pm = newP
+        rows = [
+            column(row, 0) * rows[0]
+            + column(row, 1) * rows[1]
+            + (column(row, 2) * rows[2] + unit[3] * row)
+            for row in rows
+        ]
+    q = [column(row, 3) for row in rows]
     out = []
     for k in range(3):
         total = None
@@ -252,7 +251,7 @@
                 :,
             ],
             send_sem=send_sem,
-            recv_sem=recv_sems.at[jnp.where(relayed, ROUNDS, 0)],
+            recv_sem=recv_sems.at[jnp.where(relayed, ROUNDS + slot, 0)],
             device_id=(jnp.where(relayed, RELAY_A, near(OFFSETS[q])),),
             device_id_type=MESH,
         ).start()
@@ -266,7 +265,7 @@
             src_ref=here,
             dst_ref=xs[0].at[pl.ds(pl.multiple_of(row, 8), GMAX), :],
             send_sem=relay_sem,
-            recv_sem=recv_sems.at[jnp.where(first, ROUNDS, 0)],
+            recv_sem=recv_sems.at[jnp.where(first, ROUNDS + i, 0)],
             device_id=(jnp.where(first, RELAY_B, ndev - before_end),),
             device_id_type=MESH,
         )
@@ -276,8 +275,9 @@
 
     @pl.when(is_relay)
     def _():
-        pltpu.make_async_copy(relay_part, relay_part, recv_sems.at[ROUNDS]).wait()
         for i in range(len(RELAYED)):
+            here = xs[0].at[pl.ds(RELAY_ROW + i * GMAX, GMAX), :]
+            pltpu.make_async_copy(here, here, recv_sems.at[ROUNDS + i]).wait()
             forward(i).start()
 
     for x in xs:
@@ -357,7 +357,7 @@
             parts = [a + b for a, b in zip(parts[::2], parts[1::2])]
         total = parts[0]
         return {
-            pair: jnp.broadcast_to(total[:, e : e + 1], (1, BLK)) for e, pair in enumerate(PAIRS)
+            pair: jnp.broadcast_to(total[:, e : e + 1], (8, BLK)) for e, pair in enumerate(PAIRS)
         }
 
     def meet(step):
@@ -366,7 +366,11 @@
 
     zero_row = jnp.zeros((1, BLK), jnp.float32)
     meet(0)
-    substep = jnp.full((1, BLK), step_s[0] * 0.5, jnp.float32)
+    substep = jnp.full((8, BLK), step_s[0] * 0.5, jnp.float32)
+
+    def times(c, field):
+        return (field.reshape(BDEV // 8, 8, BLK) * c[None]).reshape(BDEV, BLK)
+
     us = None
     for r in range(1, ROUNDS):
         if r <= 4:
@@ -390,18 +394,24 @@
                     term = -low if term is None else term - low
                 d[k] = term
             d[0] = d[0] + 1.0
-            us = [d[0] * w[k] + d[1] * w[k + 1] + d[2] * w[k + 2] + d[3] * w[k + 3] for k in range(3)]
-            tail = d[0] * w[3] + d[1] * w[4] + d[2] * w[5]
+            us = [
+                times(d[0], w[k]) + times(d[1], w[k + 1]) + times(d[2], w[k + 2]) + times(d[3], w[k + 3])
+                for k in range(3)
+            ]
+            tail = times(d[0], w[3]) + times(d[1], w[4]) + times(d[2], w[5])
             partial = sums_row([us[i] * us[j] for i, j in PAIRS[:6]], 0, zero_row)
             base = (
-                conc[...] + first_weights[0] * w[0] + first_weights[1] * w[1] + first_weights[2] * w[2]
+                conc[...]
+                + times(first_weights[0], w[0])
+                + times(first_weights[1], w[1])
+                + times(first_weights[2], w[2])
             )
         await_ghosts(r)
         turn(r)
-    last = tail + d[3] * ys[ROUNDS - 1]
+    last = tail + times(d[3], ys[ROUNDS - 1])
     broadcast_gram(1, sums_row([us[i] * last for i in range(3)], 6, partial))
     second = arnoldi_weights(collect_gram(1), substep)
-    ordered[...] = base + second[0] * us[0] + second[1] * us[1] + second[2] * us[2]
+    ordered[...] = base + times(second[0], us[0]) + times(second[1], us[1]) + times(second[2], us[2])
     for b in range(BDEV):
         result[pl.ds(b, 1), :] = ordered[pl.ds(place_s[b], 1), :]
     pltpu.make_async_copy(sends, sends, send_sem).wait()
@@ -422,7 +432,7 @@
         return pl.pallas_call(
             lambda *refs: kernel(ndev, *refs),
             out_shape=pltpu.VMEM((BDEV, BLK), f32),
-            in_specs=[pl.BlockSpec(memory_space=pl.ANY)] * 7,
+            in_specs=[pl.BlockSpec(memory_space=pltpu.HBM)] * 7,
             out_specs=pl.BlockSpec(memory_space=pltpu.VMEM),
             scratch_shapes=[
                 pltpu.VMEM((BDEV, BLK), f32),
@@ -452,7 +462,7 @@
                 pltpu.SemaphoreType.DMA((6,)),
                 pltpu.SemaphoreType.DMA,
                 pltpu.SemaphoreType.DMA,
-                pltpu.SemaphoreType.DMA((ROUNDS + 1,)),
+                pltpu.SemaphoreType.DMA((ROUNDS + len(RELAYED),)),
                 pltpu.SemaphoreType.DMA,
                 pltpu.SemaphoreType.DMA((2,)),
                 pltpu.SemaphoreType.DMA,

time: 54 us -> 53.5 us (level)
  no operation moved by 1% of the time
where the time goes in v6:
time: 53.5 us; the launch traced here: 53.4 us
  Pallas kernels  52.1 us (97%)
  between operations  0.66 us (1%)
  local copies, waits for them, and re-layouts  0.61 us (1%)
    pallas_call x1, Pallas kernels, step(): pl.pallas_call(lambda *refs: kernel(ndev, *refs), out_shape=pltpu.VMEM((B...  52.1 us

profile of v6, /device:TPU:1, one launch (start us, length us, event | category | flops | bytes accessed | tf_op | source)
XLA Modules:
  0.0 53.4 jit_solution(8210426573485759615)
XLA Ops:
  0.7 52.1 %rosenbrock.1 = f32[32,128]{1,0:T(8,128)S(1)} custom-call(f32[32,128]{1,0:T(8,128)} %refs_0_.1, f32[32,128]{1,0:T(8,128)} %refs_1_.1, f32[1]{0:T(128)S(6)} %copy.10.refs_2_, f32[32,5,128,128]{3,2,1,0:T(8,128)} %refs_3_.1, s32[5,32]{1,0:T(8,128)} %bitcast.1, s32[32]{0:T(128)} %refs_5_.1, s32[1,4,16]{2,1,0:T(4,128)} %refs_6_.1), custom_call_target="tpu_custom_call" | custom-call | tf_op jit(solution)/shard_map/rosenbrock/pallas_call | solution.py:432
  52.8 0.6 %copy.9 = f32[32,128]{1,0:T(8,128)} copy(f32[32,128]{1,0:T(8,128)S(1)} %rosenbrock.1) | data formatting | bytes 32768

commit v7 on v6

--- a/solution.py
+++ b/solution.py
@@ -118,8 +118,9 @@
 def kernel(ndev, conc_hbm, rate_hbm, step_hbm, blocks_hbm, cols_hbm, lens_hbm, lists_hbm, result, *scratch):
     (conc_in, rate_in, conc, rate, slope8, fixed, blocks, ys, sends, gram_row, arrivals, ordered) = scratch[:12]
     (step_s, cols_s, lens_s, lists_s, index_s, place_s, row_s, pick_s) = scratch[12:20]
-    xs = scratch[20 : 20 + ROUNDS]
-    in_sems, block_sem, send_sem, recv_sems, ar_send, ar_recv, relay_sem, known = scratch[20 + ROUNDS :]
+    stacked, folded, us_ref = scratch[20:23]
+    xs = scratch[23 : 23 + ROUNDS]
+    in_sems, block_sem, send_sem, recv_sems, ar_send, ar_recv, relay_sem, known = scratch[23 + ROUNDS :]
     me = lax.axis_index("dom")
 
     def near(o):
@@ -216,6 +217,25 @@
             ys[r, pl.ds(p, 1), :] = whole
             if r + 1 < ROUNDS:
                 xs[r + 1][pl.ds(p, 1), :] = whole
+
+    def fold():
+        def split(value):
+            high = value.astype(jnp.bfloat16)
+            return high, (value - high.astype(jnp.float32)).astype(jnp.bfloat16)
+
+        def group(i, carry):
+            for s in range(GROUP):
+                p = i * GROUP + s
+                left = jnp.concatenate(split(stacked[p]), axis=0)
+                for t in range(1, NNZB):
+                    right = jnp.concatenate(split(blocks[row_s[p], t]), axis=1)
+                    both = jnp.dot(left, right, preferred_element_type=jnp.float32)
+                    folded[p * NNZB + t] = (
+                        both[:8, :BLK] + both[:8, BLK:] + (both[8:, :BLK] + both[8:, BLK:])
+                    )
+            return carry
+
+        lax.fori_loop(0, BDEV // GROUP, group, 0)
 
     def turn(r):
         product(r, 0, GMAX)
@@ -282,6 +302,7 @@
 
     for x in xs:
         x[pl.ds(ZERO_ROW, 8), :] = jnp.zeros((8, BLK), jnp.float32)
+    stacked[...] = jnp.zeros_like(stacked)
     for copy in small[2:]:
         copy.wait()
 
@@ -328,6 +349,7 @@
     turn(0)
 
     lane = lax.broadcasted_iota(jnp.int32, (1, BLK), 1)
+    sublane = lax.broadcasted_iota(jnp.int32, (8, BLK), 0)
 
     def sums_row(products, first, row):
         for e, p in enumerate(products, first):
@@ -400,6 +422,17 @@
             ]
             tail = times(d[0], w[3]) + times(d[1], w[4]) + times(d[2], w[5])
             partial = sums_row([us[i] * us[j] for i, j in PAIRS[:6]], 0, zero_row)
+            for k in range(3):
+                us_ref[k] = us[k]
+            for p in range(BDEV):
+                for k in range(3):
+                    stacked[p, pl.ds(k, 1), :] = us_ref[k, pl.ds(p, 1), :]
+            fold()
+            kept = []
+            for k in range(3):
+                mine = us[k] * (tail + times(d[3], fixed[...]) * SCALE)
+                kept.append(jnp.sum(mine, axis=0, keepdims=True))
+            known_part = jnp.concatenate(kept + [jnp.zeros((5, BLK), jnp.float32)], axis=0)
             base = (
                 conc[...]
                 + times(first_weights[0], w[0])
@@ -407,9 +440,21 @@
                 + times(first_weights[2], w[2])
             )
         await_ghosts(r)
-        turn(r)
-    last = tail + times(d[3], ys[ROUNDS - 1])
-    broadcast_gram(1, sums_row([us[i] * last for i in range(3)], 6, partial))
+        if r < ROUNDS - 1:
+            turn(r)
+    x = xs[ROUNDS - 1]
+    parts = [None] * 8
+    for p in range(BDEV):
+        for t in range(1, NNZB):
+            term = folded[p * NNZB + t] * x[pl.ds(index_s[p * NNZB + t], 8, stride=0), :]
+            i = (p * 4 + t) % 8
+            parts[i] = term if parts[i] is None else parts[i] + term
+    while len(parts) > 1:
+        parts = [a + b for a, b in zip(parts[::2], parts[1::2])]
+    late = jnp.sum(known_part - d[3] * SCALE * parts[0], axis=1, keepdims=True)
+    diagonal = lax.broadcasted_iota(jnp.int32, (8, BLK), 1) == sublane + 6
+    inner = jnp.where(diagonal & (sublane < 3), late, 0.0)
+    broadcast_gram(1, partial + jnp.sum(inner, axis=0, keepdims=True))
     second = arnoldi_weights(collect_gram(1), substep)
     ordered[...] = base + times(second[0], us[0]) + times(second[1], us[1]) + times(second[2], us[2])
     for b in range(BDEV):
@@ -455,6 +500,11 @@
                 pltpu.SMEM((ZERO_ROW,), i32),
                 pltpu.SMEM((BDEV,), i32),
                 pltpu.SMEM((4 * GMAX,), i32),
+            ]
+            + [
+                pltpu.VMEM((BDEV, 8, BLK), f32),
+                pltpu.VMEM((BDEV * NNZB, 8, BLK), f32),
+                pltpu.VMEM((3, BDEV, BLK), f32),
             ]
             + [pltpu.VMEM((XROWS + len(RELAYED) * GMAX, BLK), f32)]
             + [pltpu.VMEM((XROWS, BLK), f32)] * (ROUNDS - 1)

time: 53.5 us -> 53 us (level)
  no operation moved by 1% of the time
where the time goes in v7:
time: 53 us; the launch traced here: 52.9 us
  Pallas kernels  51.6 us (97%)
  between operations  0.66 us (1%)
  local copies, waits for them, and re-layouts  0.61 us (1%)
    pallas_call x1, Pallas kernels, step(): pl.pallas_call(lambda *refs: kernel(ndev, *refs), out_shape=pltpu.VMEM((B...  51.6 us

profile of v7, /device:TPU:1, one launch (start us, length us, event | category | flops | bytes accessed | tf_op | source)
XLA Modules:
  0.0 52.9 jit_solution(16341324803623548736)
XLA Ops:
  0.7 51.6 %rosenbrock.1 = f32[32,128]{1,0:T(8,128)S(1)} custom-call(f32[32,128]{1,0:T(8,128)} %refs_0_.1, f32[32,128]{1,0:T(8,128)} %refs_1_.1, f32[1]{0:T(128)S(6)} %copy.10.refs_2_, f32[32,5,128,128]{3,2,1,0:T(8,128)} %refs_3_.1, s32[5,32]{1,0:T(8,128)} %bitcast.1, s32[32]{0:T(128)} %refs_5_.1, s32[1,4,16]{2,1,0:T(4,128)} %refs_6_.1), custom_call_target="tpu_custom_call" | custom-call | tf_op jit(solution)/shard_map/rosenbrock/pallas_call | solution.py:477
  52.2 0.6 %copy.9 = f32[32,128]{1,0:T(8,128)} copy(f32[32,128]{1,0:T(8,128)S(1)} %rosenbrock.1) | data formatting | bytes 32768

commit v8 on v7

--- a/solution.py
+++ b/solution.py
@@ -19,6 +19,7 @@
 CHUNK = 4
 ZERO_ROW = BDEV + 4 * GMAX
 XROWS = ZERO_ROW + 8
+MATRIX = 4
 RELAY_ROW = XROWS
 RELAY_A = 7
 RELAY_B = 103
@@ -118,9 +119,9 @@
 def kernel(ndev, conc_hbm, rate_hbm, step_hbm, blocks_hbm, cols_hbm, lens_hbm, lists_hbm, result, *scratch):
     (conc_in, rate_in, conc, rate, slope8, fixed, blocks, ys, sends, gram_row, arrivals, ordered) = scratch[:12]
     (step_s, cols_s, lens_s, lists_s, index_s, place_s, row_s, pick_s) = scratch[12:20]
-    stacked, folded, us_ref = scratch[20:23]
-    xs = scratch[23 : 23 + ROUNDS]
-    in_sems, block_sem, send_sem, recv_sems, ar_send, ar_recv, relay_sem, known = scratch[23 + ROUNDS :]
+    stacked, folded, us_ref, weights = scratch[20:24]
+    xs = scratch[24 : 24 + ROUNDS]
+    in_sems, block_sem, send_sem, recv_sems, ar_send, ar_recv, relay_sem, known = scratch[24 + ROUNDS :]
     me = lax.axis_index("dom")
 
     def near(o):
@@ -137,16 +138,10 @@
         pltpu.make_async_copy(rate_hbm, rate_in, in_sems.at[4]),
         pltpu.make_async_copy(step_hbm, step_s, in_sems.at[5]),
     ]
-    for copy in small:
-        copy.start()
-
     barrier = pltpu.get_barrier_semaphore()
 
     def greet(device):
         pl.semaphore_signal(barrier, inc=1, device_id=(device,), device_id_type=MESH)
-
-    for q in ORDER:
-        greet(jnp.where(me + OFFSETS[q] >= ndev, RELAY_B, near(OFFSETS[q])))
 
     @pl.when(me == RELAY_A)
     def _():
@@ -156,6 +151,12 @@
     @pl.when(me == RELAY_B)
     def _():
         greet(RELAY_A)
+
+    for q in ORDER:
+        greet(jnp.where(me + OFFSETS[q] >= ndev, RELAY_B, near(OFFSETS[q])))
+
+    for copy in small:
+        copy.start()
 
     greetings = (
         4
@@ -203,6 +204,37 @@
 
         lax.fori_loop(0, BDEV // GROUP, group, 0)
 
+    def split(value):
+        high = value.astype(jnp.bfloat16)
+        return high, (value - high.astype(jnp.float32)).astype(jnp.bfloat16)
+
+    def load_weights():
+        def one(m, carry):
+            b = row_s[GMAX - MATRIX + m]
+            for t in range(1, NNZB):
+                weights[m, pl.ds((t - 1) * BLK, BLK), :] = jnp.concatenate(split(blocks[b, t].T), axis=1)
+            return carry
+
+        lax.fori_loop(0, MATRIX, one, 0)
+
+    def keep(r, p, whole):
+        ys[r, pl.ds(p, 1), :] = whole
+        if r + 1 < ROUNDS:
+            xs[r + 1][pl.ds(p, 1), :] = whole
+
+    def matrix_product(r):
+        x = xs[r]
+        for m in range(MATRIX):
+            p = GMAX - MATRIX + m
+            wide = jnp.concatenate(
+                [x[pl.ds(index_s[p * NNZB + t], 8, stride=0), :] for t in range(1, NNZB)], axis=1
+            )
+            both = jnp.dot(
+                jnp.concatenate(split(wide), axis=0), weights[m], preferred_element_type=jnp.float32
+            )
+            row = both[:1, :BLK] + both[:1, BLK:] + (both[8:9, :BLK] + both[8:9, BLK:])
+            keep(r, p, (fixed[pl.ds(p, 1), :] - row) * SCALE)
+
     def product(r, low, high):
         x = xs[r]
         for p in range(low, high):
@@ -214,15 +246,9 @@
                 total = term if total is None else total + term
             whole = fixed[pl.ds(p, 1), :] - lane_sums(total.reshape(BLK, BLK))
             whole = whole if r == 0 else whole * SCALE
-            ys[r, pl.ds(p, 1), :] = whole
-            if r + 1 < ROUNDS:
-                xs[r + 1][pl.ds(p, 1), :] = whole
+            keep(r, p, whole)
 
     def fold():
-        def split(value):
-            high = value.astype(jnp.bfloat16)
-            return high, (value - high.astype(jnp.float32)).astype(jnp.bfloat16)
-
         def group(i, carry):
             for s in range(GROUP):
                 p = i * GROUP + s
@@ -238,7 +264,11 @@
         lax.fori_loop(0, BDEV // GROUP, group, 0)
 
     def turn(r):
-        product(r, 0, GMAX)
+        if r == 0:
+            product(r, 0, GMAX)
+        else:
+            matrix_product(r)
+            product(r, 0, GMAX - MATRIX)
         n = r + 1
         if n < ROUNDS:
             packet(n, urgent, ys.at[r, pl.ds(0, GMAX), :]).start()
@@ -395,10 +425,14 @@
 
     us = None
     for r in range(1, ROUNDS):
+        if r == 1:
+            own_part(r)
+            load_weights()
         if r <= 4:
             pl.semaphore_wait(known.at[r - 1], 2)
             meet(r)
-        own_part(r)
+        if r > 1:
+            own_part(r)
         if r == 4:
             pl.semaphore_wait(known.at[4], 2)
             w = [ys[k] for k in range(4)]
@@ -505,6 +539,7 @@
                 pltpu.VMEM((BDEV, 8, BLK), f32),
                 pltpu.VMEM((BDEV * NNZB, 8, BLK), f32),
                 pltpu.VMEM((3, BDEV, BLK), f32),
+                pltpu.VMEM((MATRIX, (NNZB - 1) * BLK, 2 * BLK), jnp.bfloat16),
             ]
             + [pltpu.VMEM((XROWS + len(RELAYED) * GMAX, BLK), f32)]
             + [pltpu.VMEM((XROWS, BLK), f32)] * (ROUNDS - 1)

time: 53 us -> 53.2 us (level)
  no operation moved by 1% of the time
where the time goes in v8:
time: 53.2 us; the launch traced here: 53.1 us
  Pallas kernels  51.8 us (97%)
  between operations  0.66 us (1%)
  local copies, waits for them, and re-layouts  0.61 us (1%)
    pallas_call x1, Pallas kernels, step(): pl.pallas_call(lambda *refs: kernel(ndev, *refs), out_shape=pltpu.VMEM((B...  51.8 us

profile of v8, /device:TPU:1, one launch (start us, length us, event | category | flops | bytes accessed | tf_op | source)
XLA Modules:
  0.0 53.1 jit_solution(8372123224499707231)
XLA Ops:
  0.7 51.8 %rosenbrock.1 = f32[32,128]{1,0:T(8,128)S(1)} custom-call(f32[32,128]{1,0:T(8,128)} %refs_0_.1, f32[32,128]{1,0:T(8,128)} %refs_1_.1, f32[1]{0:T(128)S(6)} %copy.10.refs_2_, f32[32,5,128,128]{3,2,1,0:T(8,128)} %refs_3_.1, s32[5,32]{1,0:T(8,128)} %bitcast.1, s32[32]{0:T(128)} %refs_5_.1, s32[1,4,16]{2,1,0:T(4,128)} %refs_6_.1), custom_call_target="tpu_custom_call" | custom-call | tf_op jit(solution)/shard_map/rosenbrock/pallas_call | solution.py:511
  52.5 0.6 %copy.9 = f32[32,128]{1,0:T(8,128)} copy(f32[32,128]{1,0:T(8,128)S(1)} %rosenbrock.1) | data formatting | bytes 32768

commit v9 on v8

--- a/solution.py
+++ b/solution.py
@@ -138,6 +138,9 @@
         pltpu.make_async_copy(rate_hbm, rate_in, in_sems.at[4]),
         pltpu.make_async_copy(step_hbm, step_s, in_sems.at[5]),
     ]
+    for copy in small:
+        copy.start()
+
     barrier = pltpu.get_barrier_semaphore()
 
     def greet(device):
@@ -154,9 +157,6 @@
 
     for q in ORDER:
         greet(jnp.where(me + OFFSETS[q] >= ndev, RELAY_B, near(OFFSETS[q])))
-
-    for copy in small:
-        copy.start()
 
     greetings = (
         4

time: 53.2 us -> 52.8 us (level)
  no operation moved by 1% of the time
where the time goes in v9:
time: 52.8 us; the launch traced here: 52.7 us
  Pallas kernels  51.4 us (97%)
  between operations  0.66 us (1%)
  local copies, waits for them, and re-layouts  0.61 us (1%)
    pallas_call x1, Pallas kernels, step(): pl.pallas_call(lambda *refs: kernel(ndev, *refs), out_shape=pltpu.VMEM((B...  51.4 us

profile of v9, /device:TPU:1, one launch (start us, length us, event | category | flops | bytes accessed | tf_op | source)
XLA Modules:
  0.0 52.7 jit_solution(3167753970641011894)
XLA Ops:
  0.7 51.4 %rosenbrock.1 = f32[32,128]{1,0:T(8,128)S(1)} custom-call(f32[32,128]{1,0:T(8,128)} %refs_0_.1, f32[32,128]{1,0:T(8,128)} %refs_1_.1, f32[1]{0:T(128)S(6)} %copy.10.refs_2_, f32[32,5,128,128]{3,2,1,0:T(8,128)} %refs_3_.1, s32[5,32]{1,0:T(8,128)} %bitcast.1, s32[32]{0:T(128)} %refs_5_.1, s32[1,4,16]{2,1,0:T(4,128)} %refs_6_.1), custom_call_target="tpu_custom_call" | custom-call | tf_op jit(solution)/shard_map/rosenbrock/pallas_call | solution.py:511
  52.0 0.6 %copy.9 = f32[32,128]{1,0:T(8,128)} copy(f32[32,128]{1,0:T(8,128)S(1)} %rosenbrock.1) | data formatting | bytes 32768

commit v10 on v9

--- a/solution.py
+++ b/solution.py
@@ -116,12 +116,12 @@
     return out
 
 
-def kernel(ndev, conc_hbm, rate_hbm, step_hbm, blocks_hbm, cols_hbm, lens_hbm, lists_hbm, result, *scratch):
+def kernel(ndev, conc_hbm, rate_hbm, step_ref, blocks_hbm, cols_hbm, lens_hbm, lists_hbm, result, *scratch):
     (conc_in, rate_in, conc, rate, slope8, fixed, blocks, ys, sends, gram_row, arrivals, ordered) = scratch[:12]
-    (step_s, cols_s, lens_s, lists_s, index_s, place_s, row_s, pick_s) = scratch[12:20]
-    stacked, folded, us_ref, weights = scratch[20:24]
-    xs = scratch[24 : 24 + ROUNDS]
-    in_sems, block_sem, send_sem, recv_sems, ar_send, ar_recv, relay_sem, known = scratch[24 + ROUNDS :]
+    (cols_s, lens_s, lists_s, index_s, place_s, row_s, pick_s) = scratch[12:19]
+    stacked, folded, us_ref, weights = scratch[19:23]
+    xs = scratch[23 : 23 + ROUNDS]
+    in_sems, block_sem, send_sem, recv_sems, ar_send, ar_recv, relay_sem, known = scratch[23 + ROUNDS :]
     me = lax.axis_index("dom")
 
     def near(o):
@@ -136,11 +136,7 @@
         pltpu.make_async_copy(cols_hbm, cols_s, in_sems.at[2]),
         pltpu.make_async_copy(lens_hbm, lens_s, in_sems.at[3]),
         pltpu.make_async_copy(rate_hbm, rate_in, in_sems.at[4]),
-        pltpu.make_async_copy(step_hbm, step_s, in_sems.at[5]),
     ]
-    for copy in small:
-        copy.start()
-
     barrier = pltpu.get_barrier_semaphore()
 
     def greet(device):
@@ -154,6 +150,9 @@
     @pl.when(me == RELAY_B)
     def _():
         greet(RELAY_A)
+
+    for copy in small:
+        copy.start()
 
     for q in ORDER:
         greet(jnp.where(me + OFFSETS[q] >= ndev, RELAY_B, near(OFFSETS[q])))
@@ -418,7 +417,7 @@
 
     zero_row = jnp.zeros((1, BLK), jnp.float32)
     meet(0)
-    substep = jnp.full((8, BLK), step_s[0] * 0.5, jnp.float32)
+    substep = jnp.full((8, BLK), step_ref[0] * 0.5, jnp.float32)
 
     def times(c, field):
         return (field.reshape(BDEV // 8, 8, BLK) * c[None]).reshape(BDEV, BLK)
@@ -511,7 +510,9 @@
         return pl.pallas_call(
             lambda *refs: kernel(ndev, *refs),
             out_shape=pltpu.VMEM((BDEV, BLK), f32),
-            in_specs=[pl.BlockSpec(memory_space=pltpu.HBM)] * 7,
+            in_specs=[pl.BlockSpec(memory_space=pltpu.HBM)] * 2
+            + [pl.BlockSpec(memory_space=pltpu.SMEM)]
+            + [pl.BlockSpec(memory_space=pltpu.HBM)] * 4,
             out_specs=pl.BlockSpec(memory_space=pltpu.VMEM),
             scratch_shapes=[
                 pltpu.VMEM((BDEV, BLK), f32),
@@ -526,7 +527,6 @@
                 pltpu.VMEM((2, 1, BLK), f32),
                 pltpu.VMEM((2, ndev, 1, BLK), f32),
                 pltpu.VMEM((BDEV, BLK), f32),
-                pltpu.SMEM((1,), f32),
                 pltpu.SMEM((NNZB, BDEV), i32),
                 pltpu.SMEM((BDEV,), i32),
                 pltpu.SMEM((1, 4, GMAX), i32),
@@ -544,7 +544,7 @@
             + [pltpu.VMEM((XROWS + len(RELAYED) * GMAX, BLK), f32)]
             + [pltpu.VMEM((XROWS, BLK), f32)] * (ROUNDS - 1)
             + [
-                pltpu.SemaphoreType.DMA((6,)),
+                pltpu.SemaphoreType.DMA((5,)),
                 pltpu.SemaphoreType.DMA,
                 pltpu.SemaphoreType.DMA,
                 pltpu.SemaphoreType.DMA((ROUNDS + len(RELAYED),)),

time: 52.8 us -> 52.8 us (level)
  no operation moved by 1% of the time
where the time goes in v10:
time: 52.8 us; the launch traced here: 52.7 us
  Pallas kernels  51.4 us (97%)
  between operations  0.66 us (1%)
  local copies, waits for them, and re-layouts  0.61 us (1%)
    pallas_call x1, Pallas kernels, step(): pl.pallas_call(lambda *refs: kernel(ndev, *refs), out_shape=pltpu.VMEM((B...  51.4 us

profile of v10, /device:TPU:1, one launch (start us, length us, event | category | flops | bytes accessed | tf_op | source)
XLA Modules:
  0.0 52.7 jit_solution(3010618514764601469)
XLA Ops:
  0.7 51.4 %rosenbrock.1 = f32[32,128]{1,0:T(8,128)S(1)} custom-call(f32[32,128]{1,0:T(8,128)} %refs_0_.1, f32[32,128]{1,0:T(8,128)} %refs_1_.1, f32[1]{0:T(128)S(6)} %copy.10.refs_2_, f32[32,5,128,128]{3,2,1,0:T(8,128)} %refs_3_.1, s32[5,32]{1,0:T(8,128)} %bitcast.1, s32[32]{0:T(128)} %refs_5_.1, s32[1,4,16]{2,1,0:T(4,128)} %refs_6_.1), custom_call_target="tpu_custom_call" | custom-call | tf_op jit(solution)/shard_map/rosenbrock/pallas_call | solution.py:510
  52.0 0.6 %copy.9 = f32[32,128]{1,0:T(8,128)} copy(f32[32,128]{1,0:T(8,128)S(1)} %rosenbrock.1) | data formatting | bytes 32768

commit v11 on v9

--- a/solution.py
+++ b/solution.py
@@ -175,14 +175,14 @@
             src_ref=source,
             dst_ref=xs[r].at[pl.ds(pl.multiple_of(BDEV + q * GMAX, 8), GMAX), :],
             send_sem=send_sem,
-            recv_sem=recv_sems.at[r],
+            recv_sem=recv_sems.at[r % 2],
             device_id=(lax.rem(me + offset + ndev, ndev),),
             device_id_type=MESH,
         )
 
     def await_ghosts(r):
         part = xs[r].at[pl.ds(BDEV, 4 * GMAX), :]
-        pltpu.make_async_copy(part, part, recv_sems.at[r]).wait()
+        pltpu.make_async_copy(part, part, recv_sems.at[r % 2]).wait()
 
     def lane_sums(total):
         return jnp.sum(total.T, axis=0, keepdims=True)
@@ -301,7 +301,7 @@
                 :,
             ],
             send_sem=send_sem,
-            recv_sem=recv_sems.at[jnp.where(relayed, ROUNDS + slot, 0)],
+            recv_sem=recv_sems.at[jnp.where(relayed, 2 + slot, 0)],
             device_id=(jnp.where(relayed, RELAY_A, near(OFFSETS[q])),),
             device_id_type=MESH,
         ).start()
@@ -315,7 +315,7 @@
             src_ref=here,
             dst_ref=xs[0].at[pl.ds(pl.multiple_of(row, 8), GMAX), :],
             send_sem=relay_sem,
-            recv_sem=recv_sems.at[jnp.where(first, ROUNDS + i, 0)],
+            recv_sem=recv_sems.at[jnp.where(first, 2 + i, 0)],
             device_id=(jnp.where(first, RELAY_B, ndev - before_end),),
             device_id_type=MESH,
         )
@@ -327,7 +327,7 @@
     def _():
         for i in range(len(RELAYED)):
             here = xs[0].at[pl.ds(RELAY_ROW + i * GMAX, GMAX), :]
-            pltpu.make_async_copy(here, here, recv_sems.at[ROUNDS + i]).wait()
+            pltpu.make_async_copy(here, here, recv_sems.at[2 + i]).wait()
             forward(i).start()
 
     for x in xs:
@@ -547,7 +547,7 @@
                 pltpu.SemaphoreType.DMA((6,)),
                 pltpu.SemaphoreType.DMA,
                 pltpu.SemaphoreType.DMA,
-                pltpu.SemaphoreType.DMA((ROUNDS + len(RELAYED),)),
+                pltpu.SemaphoreType.DMA((2 + len(RELAYED),)),
                 pltpu.SemaphoreType.DMA,
                 pltpu.SemaphoreType.DMA((2,)),
                 pltpu.SemaphoreType.DMA,

time: 52.8 us -> 52.7 us (level)
  no operation moved by 1% of the time
where the time goes in v11:
time: 52.7 us; the launch traced here: 52.6 us
  Pallas kernels  51.3 us (97%)
  between operations  0.66 us (1%)
  local copies, waits for them, and re-layouts  0.61 us (1%)
    pallas_call x1, Pallas kernels, step(): pl.pallas_call(lambda *refs: kernel(ndev, *refs), out_shape=pltpu.VMEM((B...  51.3 us

profile of v11, /device:TPU:1, one launch (start us, length us, event | category | flops | bytes accessed | tf_op | source)
XLA Modules:
  0.0 52.6 jit_solution(18050191345085618105)
XLA Ops:
  0.7 51.3 %rosenbrock.1 = f32[32,128]{1,0:T(8,128)S(1)} custom-call(f32[32,128]{1,0:T(8,128)} %refs_0_.1, f32[32,128]{1,0:T(8,128)} %refs_1_.1, f32[1]{0:T(128)S(6)} %copy.10.refs_2_, f32[32,5,128,128]{3,2,1,0:T(8,128)} %refs_3_.1, s32[5,32]{1,0:T(8,128)} %bitcast.1, s32[32]{0:T(128)} %refs_5_.1, s32[1,4,16]{2,1,0:T(4,128)} %refs_6_.1), custom_call_target="tpu_custom_call" | custom-call | tf_op jit(solution)/shard_map/rosenbrock/pallas_call | solution.py:511
  52.0 0.6 %copy.9 = f32[32,128]{1,0:T(8,128)} copy(f32[32,128]{1,0:T(8,128)S(1)} %rosenbrock.1) | data formatting | bytes 32768
